TPU v7x, 32 devices: a whole 2x2x4 slice. The times are simulated.
32 devices in a mesh: pop: 8 (over z, y), mp: 4 (over x, core).
Axes of the slice: x: 2, y: 2, z: 4, core: 2. Of those that a mesh axis runs over, the one named last changes fastest.
Arguments:
- token_ids: int32 [96, 4, 16], P('pop'), may hold values from 0 to 255
- fitness_ranks: int32 [96], P('pop'), may hold values from 0 to 143, as said below
- embedding: bfloat16 [256, 4096], P(None, 'mp'), may hold values from -6 to 6
- mix_weights: bfloat16 [2, 4096, 4096], P(None, 'mp'), may hold values from -0.09375 to 0.09375
- factors_in: bfloat16 [2, 96, 4, 4096], P(None, 'pop', None, 'mp'), may hold values from -6 to 6
- factors_out: bfloat16 [2, 96, 4, 4096], P(None, 'pop'), may hold values from -6 to 6
- decay_rates: float32 [2, 4096], P(None, 'mp'), may hold values from 0.2 to 0.98
- norm_gain: float32 [2, 4096], P(None, 'mp'), may hold values from 0.1 to 1.9
- reward_dir: float32 [4096], P('mp'), may hold values from -6 to 6
Outputs:
- final_features: bfloat16 [96, 4, 4096], P('pop', None, 'mp')
- scores: float32 [96, 4], P('pop')
- weight_step: float32 [2, 4096, 4096], P(None, 'mp', 'pop')
Inputs may be any that keep to these rules, and one draw needn't show every extreme that they name: `fitness_ranks`: ranks may repeat.
All inputs are finite; a program needn't handle non-finite values.
Results may differ from a plain program's by a relative error of at most 0.023.
Values may be sent and summed in bfloat16 or wider, within the bound.
A program may use at most 128 MiB of HBM per device.

v0:
```python
import functools

import jax
import jax.numpy as jnp
from jax import lax
from jax.experimental import pallas as pl
from jax.experimental.pallas import tpu as pltpu
from jax.sharding import PartitionSpec as P

noise_scale = 0.25
norm_eps = 1e-06
spread_eps = 1e-05
lanes = 128
f32, bf16 = jnp.float32, jnp.bfloat16


def policy_kernel(
    dims,
    ids_ref,
    embed_ref,
    mix_ref,
    fin_raw,
    fout_hbm,
    ranks_smem,
    decay_ref,
    gain_ref,
    reward_ref,
    final_ref,
    score_ref,
    gin_ref,
    gout_ref,
    weights,
    own_pair,
    got_pair,
    own_cross,
    got_cross,
    states,
    hidden,
    onehot_ref,
    fout_raw,
    fin_ref,
    fout_ref,
    scaled,
    ranks,
    granks_ref,
    lows,
    squares,
    small,
    marks,
    weight_sem,
    pair_send,
    pair_recv,
    cross_send,
    cross_recv,
    small_send,
    small_recv,
    mark_send,
    mark_recv,
    pop_send,
    pop_recv,
    self_sem,
    load_sem,
):
    pop, chunks, group, steps, member_rows, seqs, rank, width, full, coef = dims
    parts = pair_send.shape[2]
    piece = width // parts
    halves = [slice(p * piece, (p + 1) * piece) for p in range(parts)]
    rows = group * steps
    vocab = embed_ref.shape[0]
    local = fin_ref.shape[1]
    columns = gout_ref.shape[2]
    mine = lax.axis_index("pop")
    me = lax.axis_index("mp")
    side, core = me // 2, me % 2
    mate = side * 2 + (1 - core)
    cross = (1 - side) * 2 + core
    diagonal = (1 - side) * 2 + (1 - core)
    others = (mate, cross, diagonal)
    blocks = (diagonal, cross, mate, me)

    def peer(q, j):
        return {"pop": q, "mp": j}

    def remote(src, dst, send, recv, q, j):
        return pltpu.make_async_remote_copy(
            src_ref=src,
            dst_ref=dst,
            send_sem=send,
            recv_sem=recv,
            device_id=peer(q, j),
            device_id_type=pl.DeviceIdType.MESH,
        )

    def weight_copy(layer, slot):
        start = pl.multiple_of(blocks[slot] * width, lanes)
        return pltpu.make_async_copy(
            mix_ref.at[layer, :, pl.ds(start, width)],
            weights.at[layer, slot],
            weight_sem.at[layer, slot],
        )

    for slot in range(4):
        weight_copy(0, slot).start()
    fout_load = pltpu.make_async_copy(fout_hbm, fout_raw, load_sem)
    fout_load.start()

    barrier = pltpu.get_barrier_semaphore()
    for other in others:
        pl.semaphore_signal(
            barrier, inc=1, device_id=peer(mine, other), device_id_type=pl.DeviceIdType.MESH
        )

    def greet(hop, carry):
        pl.semaphore_signal(
            barrier,
            inc=1,
            device_id=peer(lax.rem(mine + hop, pop), me),
            device_id_type=pl.DeviceIdType.MESH,
        )
        return carry

    lax.fori_loop(1, pop, greet, 0)
    pl.semaphore_wait(barrier, 3 + pop - 1)

    members = ranks_smem.shape[0]
    members_all = members * pop

    def rank_copy(hop, source):
        return remote(
            ranks,
            granks_ref.at[source],
            pop_send.at[2, hop],
            pop_recv.at[2, hop],
            lax.rem(mine + hop, pop),
            me,
        )

    def out_copy(hop, source):
        target = lax.rem(mine + hop, pop)
        at = pl.multiple_of(source * local, local)
        cols = pl.multiple_of(target * columns, lanes)
        return remote(
            fout_ref.at[:, :, pl.ds(cols, columns)],
            gout_ref.at[:, pl.ds(at, local), :],
            pop_send.at[1, hop],
            pop_recv.at[1, hop],
            target,
            me,
        )

    def in_copy(hop, source):
        at = pl.multiple_of(source * local, local)
        return remote(
            scaled,
            gin_ref.at[:, pl.ds(at, local), :],
            pop_send.at[0, hop],
            pop_recv.at[0, hop],
            lax.rem(mine + hop, pop),
            me,
        )

    def self_copies():
        at = pl.multiple_of(mine * local, local)
        cols = pl.multiple_of(mine * columns, lanes)
        return (
            pltpu.make_async_copy(scaled, gin_ref.at[:, pl.ds(at, local), :], self_sem.at[0]),
            pltpu.make_async_copy(
                fout_ref.at[:, :, pl.ds(cols, columns)],
                gout_ref.at[:, pl.ds(at, local), :],
                self_sem.at[1],
            ),
        )

    def send_with(make):
        def send(hop, carry):
            make(hop, mine).start()
            return carry

        lax.fori_loop(1, pop, send, 0)

    def rank_block(shape, axis, repeats):
        index = lax.broadcasted_iota(jnp.int32, shape, axis)
        block = jnp.zeros(shape, jnp.int32)
        for m in range(members):
            block = jnp.where(index // repeats == m, ranks_smem[m], block)
        return block

    ranks[...] = rank_block((8, lanes), 1, 1)
    send_with(rank_copy)
    granks_ref[mine] = ranks[...]

    def unpack(g, carry):
        at = pl.ds(pl.multiple_of(g * member_rows * rank, member_rows * rank), member_rows * rank)
        for layer in range(2):
            for raw, ref in ((fin_raw, fin_ref), (fout_raw, fout_ref)):
                ref[layer, at, :] = jnp.concatenate(
                    [raw[layer, g * member_rows + m].astype(f32) for m in range(member_rows)],
                    axis=0,
                ).astype(bf16)
        return carry

    def shape_ranks():
        def arrived(hop, carry):
            rank_copy(hop, lax.rem(mine + pop - hop, pop)).wait_recv()
            return carry

        lax.fori_loop(1, pop, arrived, 0)
        full_block = (pop, 8, lanes)
        kept = (lax.broadcasted_iota(jnp.int32, full_block, 1) == 0) & (
            lax.broadcasted_iota(jnp.int32, full_block, 2) < members
        )
        shares = jnp.where(kept, granks_ref[...].astype(f32) / members_all, 0.0)

        def mean_of(value):
            value = jnp.sum(value, axis=0)
            value = jnp.sum(value, axis=0, keepdims=True)
            return jnp.sum(value, axis=1, keepdims=True) / members_all

        rank_mean = mean_of(shares)
        apart = jnp.where(kept, shares - rank_mean[None], 0.0)
        spread = mean_of(apart * apart) + spread_eps
        own = rank_block((local, lanes), 0, rank).astype(f32) / members_all
        shaped = (own - rank_mean) * lax.rsqrt(spread)
        shaped = jnp.concatenate([shaped] * (width // lanes), axis=1)
        for layer in range(2):
            scaled[layer] = (fin_ref[layer].astype(f32) * shaped).astype(bf16)

    def small_copy(kind, g, r):
        return remote(
            small.at[kind, g, 0],
            small.at[kind, g, r + 1],
            small_send.at[kind, g, r],
            small_recv.at[kind, g, r],
            mine,
            others[r],
        )

    def small_start(kind, g, value):
        small[kind, g, 0] = value
        for r in range(3):
            small_copy(kind, g, r).start()

    def small_sum(kind, g):
        for r in range(3):
            small_copy(kind, g, r).wait_recv()
        return (small[kind, g, 0] + small[kind, g, 1]) + (small[kind, g, 2] + small[kind, g, 3])

    def pair_copy(k, slot, p):
        return remote(
            own_pair.at[k, slot, p],
            got_pair.at[k, slot, p],
            pair_send.at[k, slot, p],
            pair_recv.at[k, slot, p],
            mine,
            mate,
        )

    def cross_copy(k, p):
        return remote(
            own_cross.at[k, p],
            got_cross.at[k, p],
            cross_send.at[k, p],
            cross_recv.at[k, p],
            mine,
            cross,
        )

    def mark_copy(g, r):
        return remote(
            marks.at[g, 0],
            marks.at[g, r + 1],
            mark_send.at[g, r],
            mark_recv.at[g, r],
            mine,
            others[r],
        )

    def exchange(k, read, count, layer, before, put):
        def product(slot, p):
            return jnp.dot(
                read(), weights[layer, slot, :, halves[p]], preferred_element_type=f32
            ).astype(bf16)

        def summed(p):
            value = product(1, p).astype(f32)
            pair_copy(k, 0, p).wait_recv()
            own_cross[k, p, :count] = (value + got_pair[k, 0, p, :count].astype(f32)).astype(bf16)
            cross_copy(k, p).start()

        before(0)
        for p in range(parts):
            own_pair[k, 0, p, :count] = product(0, p)
            pair_copy(k, 0, p).start()
            if p == 1:
                before(1)
            if p:
                summed(p - 1)
        summed(parts - 1)
        before(2)
        for p in range(parts):
            own_pair[k, 1, p, :count] = product(2, p)
            pair_copy(k, 1, p).start()
        before(3)
        for p in range(parts):
            put(halves[p], product(3, p).astype(f32))

    def received(k, count, p):
        pair_copy(k, 1, p).wait_recv()
        cross_copy(k, p).wait_recv()
        return got_pair[k, 1, p, :count].astype(f32) + got_cross[k, p, :count].astype(f32)

    factor_rows = member_rows * rank
    mask = (lax.broadcasted_iota(jnp.int32, (factor_rows, rows), 0) // rank) == (
        (lax.broadcasted_iota(jnp.int32, (factor_rows, rows), 1) % group) // seqs
    )

    def factor_slice(ref, layer, g, start, size):
        at = pl.multiple_of(g * factor_rows, factor_rows)
        return ref[layer, pl.ds(at, factor_rows), pl.ds(start, size)]

    def low_start(layer, g, features):
        local_low = lax.dot_general(
            factor_slice(fin_ref, layer, g, 0, width),
            features,
            (((1,), (1,)), ((), ())),
            preferred_element_type=f32,
        )
        local_low = jnp.where(mask, local_low, 0.0)
        packed = local_low[:8]
        for at in range(8, factor_rows, 8):
            packed = packed + local_low[at : at + 8]
        small_start(layer, g, packed)

    def low_ready(layer, g):
        packed = small_sum(layer, g)
        low = jnp.concatenate([packed] * (factor_rows // 8), axis=0)
        low = jnp.where(mask, low, 0.0) * coef
        top = low.astype(bf16).astype(f32)
        blank = jnp.zeros((lanes - 2 * factor_rows, rows), f32)
        lows[g] = jnp.concatenate([top, low - top, blank], axis=0).T.astype(bf16)

    def correction(layer, g, p):
        start = pl.multiple_of(me * width + p * piece, lanes)
        factor = factor_slice(fout_ref, layer, g, start, piece)
        right = jnp.concatenate(
            [factor, factor, jnp.zeros((lanes - 2 * factor_rows, piece), bf16)], axis=0
        )
        return jnp.dot(lows[g], right, preferred_element_type=f32)

    def recur(layer, g, p, inputs):
        decay = decay_ref[layer : layer + 1, halves[p]]
        kept = 1.0 - decay
        carried = jnp.zeros((group, piece), f32)
        for t in range(steps):
            at = slice(t * group, (t + 1) * group)
            carried = decay * carried + kept * inputs[at]
            states[g, at, halves[p]] = carried
            powers = carried * carried
            total = powers[:, :lanes]
            for c in range(lanes, piece, lanes):
                total = total + powers[:, c : c + lanes]
            if p:
                total = total + squares[g, at, :]
            squares[g, at, :] = total

    def squares_start(layer, g):
        total = squares[g].T
        packed = total[:8]
        for at in range(8, lanes, 8):
            packed = packed + total[at : at + 8]
        small_start(2 + layer, g, packed)

    def normed(layer, g):
        squares = jnp.sum(small_sum(2 + layer, g), axis=0, keepdims=True)
        scale = lax.rsqrt(squares / full + norm_eps)
        scale = jnp.broadcast_to(scale, (lanes, rows)).T
        scale = jnp.concatenate([scale] * (width // lanes), axis=1)
        gain = gain_ref[layer : layer + 1, :]
        return (hidden[g].astype(f32) + states[g, :rows] * scale * gain).astype(bf16)

    def put_first(cols, value):
        states[0, :vocab, cols] = value

    exchange(
        0,
        lambda: embed_ref[...],
        vocab,
        0,
        lambda slot: weight_copy(0, slot).wait(),
        put_first,
    )
    for slot in range(4):
        weight_copy(1, slot).start()
    fout_load.wait()
    lax.fori_loop(0, chunks, unpack, 0)
    send_with(out_copy)

    def begin(g, carry):
        tokens = jnp.concatenate(
            [ids_ref[g * member_rows + m] for m in range(member_rows)], axis=0
        )
        entries = lax.broadcasted_iota(jnp.int32, (group, vocab), 1)
        for t in range(steps):
            onehot_ref[g, t * group : (t + 1) * group, :] = jnp.where(
                tokens[:, t : t + 1] == entries, 1.0, 0.0
            ).astype(bf16)
        features = jnp.dot(onehot_ref[g], embed_ref[...], preferred_element_type=f32).astype(bf16)
        hidden[g] = features
        low_start(0, g, features)
        return carry

    lax.fori_loop(0, chunks, begin, 0)
    shape_ranks()
    send_with(in_copy)
    for copy in self_copies():
        copy.start()
    for slot in range(4):
        weight_copy(1, slot).wait()

    def low_zero(g, carry):
        low_ready(0, g)
        return carry

    lax.fori_loop(0, chunks, low_zero, 0)
    for p in range(parts):
        whole = states[0, :vocab, halves[p]] + received(0, vocab, p)
        top = whole.astype(bf16)
        rest = (whole - top.astype(f32)).astype(bf16)

        def layer_zero(g, carry, p=p, top=top, rest=rest):
            picks = onehot_ref[g]
            inputs = (
                jnp.dot(picks, top, preferred_element_type=f32)
                + jnp.dot(picks, rest, preferred_element_type=f32)
                + correction(0, g, p)
            )
            recur(0, g, p, inputs)
            if p == parts - 1:
                squares_start(0, g)
            return carry

        for g in range(chunks):
            layer_zero(g, 0)

    def between(g, carry):
        hidden[g] = normed(0, g)

        def put(cols, value):
            states[g, :rows, cols] = value

        exchange(1 + g, lambda: hidden[g], rows, 1, lambda slot: None, put)
        low_start(1, g, hidden[g])
        return carry

    lax.fori_loop(0, chunks, between, 0)

    def layer_one(g, carry):
        low_ready(1, g)
        for p in range(parts):
            inputs = states[g, :rows, halves[p]] + received(1 + g, rows, p) + correction(1, g, p)
            recur(1, g, p, inputs)
        squares_start(1, g)
        return carry

    def finish(g, carry):
        last = normed(1, g)
        ending = last[rows - group :].astype(f32)
        for m in range(member_rows):
            final_ref[g * member_rows + m] = ending[m * seqs : (m + 1) * seqs].astype(bf16)
        total = last[:group].astype(f32)
        for t in range(1, steps):
            total = total + last[t * group : (t + 1) * group].astype(f32)
        total = total * reward_ref[...]
        packed = total[:, :lanes]
        for t in range(1, width // lanes):
            packed = packed + total[:, t * lanes : (t + 1) * lanes]
        marks[g, 0] = packed
        for r in range(3):
            mark_copy(g, r).start()
        return carry

    lax.fori_loop(0, chunks, lambda g, carry: finish(g, layer_one(g, carry)), 0)

    lane = lax.broadcasted_iota(jnp.int32, (seqs, lanes), 1)

    def collect(g, scores):
        for r in range(3):
            mark_copy(g, r).wait_recv()
        total = (marks[g, 0] + marks[g, 1]) + (marks[g, 2] + marks[g, 3])
        total = jnp.sum(total, axis=1, keepdims=True) * (full ** (-0.5) / steps)
        for m in range(member_rows):
            scores = jnp.where(
                lane == g * member_rows + m, total[m * seqs : (m + 1) * seqs], scores
            )
        for r in range(3):
            mark_copy(g, r).wait_send()
            for kind in range(4):
                small_copy(kind, g, r).wait_send()
        return scores

    score_ref[...] = lax.fori_loop(0, chunks, collect, jnp.zeros((seqs, lanes), f32))

    def drain(k, carry):
        for p in range(parts):
            pair_copy(k, 0, p).wait_send()
            pair_copy(k, 1, p).wait_send()
            cross_copy(k, p).wait_send()
        return carry

    lax.fori_loop(0, chunks + 1, drain, 0)

    def drain_pop(hop, carry):
        source = lax.rem(mine + pop - hop, pop)
        in_copy(hop, source).wait_recv()
        out_copy(hop, source).wait_recv()
        for make in (rank_copy, in_copy, out_copy):
            make(hop, mine).wait_send()
        return carry

    lax.fori_loop(1, pop, drain_pop, 0)
    for copy in self_copies():
        copy.wait()


def shards(
    token_ids,
    fitness_ranks,
    embedding,
    mix_weights,
    factors_in,
    factors_out,
    decay_rates,
    norm_gain,
    reward_dir,
):
    members, seqs, steps = token_ids.shape
    vocab, width = embedding.shape
    layers, _, full = mix_weights.shape
    rank = factors_in.shape[2]
    pop = lax.axis_size("pop")
    members_all = members * pop
    coef = noise_scale * (full * rank) ** (-0.5)
    columns = full // pop
    member_rows = 16 // seqs
    chunks = members // member_rows
    group = member_rows * seqs
    rows = group * steps
    local = members * rank
    dims = (pop, chunks, group, steps, member_rows, seqs, rank, width, full, coef)
    vmem = pl.BlockSpec(memory_space=pltpu.VMEM)
    smem = pl.BlockSpec(memory_space=pltpu.SMEM)
    hbm = pl.BlockSpec(memory_space=pl.ANY)
    most = max(rows, vocab)
    phases = chunks + 1
    parts = 4
    dma = pltpu.SemaphoreType.DMA
    final_features, marks, gin, gout = pl.pallas_call(
        functools.partial(policy_kernel, dims),
        out_shape=(
            jax.ShapeDtypeStruct((members, seqs, width), bf16),
            jax.ShapeDtypeStruct((seqs, lanes), f32),
            jax.ShapeDtypeStruct((layers, pop * local, width), bf16),
            jax.ShapeDtypeStruct((layers, pop * local, columns), bf16),
        ),
        in_specs=[vmem, vmem, hbm, vmem, hbm, smem, vmem, vmem, vmem],
        out_specs=(vmem, vmem, hbm, hbm),
        scratch_shapes=[
            pltpu.VMEM((layers, 4, width, width), bf16),
            pltpu.VMEM((phases, 2, parts, most, width // parts), bf16),
            pltpu.VMEM((phases, 2, parts, most, width // parts), bf16),
            pltpu.VMEM((phases, parts, most, width // parts), bf16),
            pltpu.VMEM((phases, parts, most, width // parts), bf16),
            pltpu.VMEM((chunks, most, width), f32),
            pltpu.VMEM((chunks, rows, width), bf16),
            pltpu.VMEM((chunks, rows, vocab), bf16),
            pltpu.VMEM((layers, members, rank, full), bf16),
            pltpu.VMEM((layers, local, width), bf16),
            pltpu.VMEM((layers, local, full), bf16),
            pltpu.VMEM((layers, local, width), bf16),
            pltpu.VMEM((8, lanes), jnp.int32),
            pltpu.VMEM((pop, 8, lanes), jnp.int32),
            pltpu.VMEM((chunks, rows, lanes), bf16),
            pltpu.VMEM((chunks, rows, lanes), f32),
            pltpu.VMEM((4, chunks, 4, 8, rows), f32),
            pltpu.VMEM((chunks, 4, group, lanes), f32),
            dma((layers, 4)),
            dma((phases, 2, parts)),
            dma((phases, 2, parts)),
            dma((phases, parts)),
            dma((phases, parts)),
            dma((4, chunks, 3)),
            dma((4, chunks, 3)),
            dma((chunks, 3)),
            dma((chunks, 3)),
            dma((3, pop)),
            dma((3, pop)),
            dma((2,)),
            dma,
        ],
        compiler_params=pltpu.CompilerParams(
            collective_id=0, has_side_effects=True, vmem_limit_bytes=60 * 1024 * 1024
        ),
    )(
        token_ids,
        embedding,
        mix_weights,
        factors_in,
        factors_out,
        fitness_ranks,
        decay_rates,
        norm_gain,
        reward_dir.reshape(1, width),
    )
    scores = marks[:, :members].T
    weight_delta = jnp.einsum("lki,lko->lio", gin, gout, preferred_element_type=f32)
    weight_step = weight_delta * (members_all * rank) ** (-0.5)
    return (final_features, scores, weight_step)


def solution(mesh):
    return jax.shard_map(
        shards,
        mesh=mesh,
        in_specs=(
            P("pop", None, None),
            P("pop"),
            P(None, "mp"),
            P(None, "mp", None),
            P(None, "pop", None, "mp"),
            P(None, "pop", None, None),
            P(None, "mp"),
            P(None, "mp"),
            P("mp"),
        ),
        out_specs=(P("pop", None, "mp"), P("pop", None), P(None, "mp", "pop")),
        check_vma=False,
    )
```

profile of v0, /device:TPU:0, one launch (start us, length us, event | category | flops | bytes accessed | tf_op | source)
XLA Modules:
  0.0 88.7 jit_solution(15229965297545629802)
XLA Ops:
  0.6 81.2 %shard_map.112 = (bf16[12,4,1024]{2,1,0:T(4,128)(2,1)}, f32[4,128]{1,0:T(4,128)}, bf16[2,384,1024]{2,1,0:T(8,128)(2,1)}, bf16[2,384,512]{2,1,0:T(8,128)(2,1)}) custom-call(s32[12,4,16]{2,1,0:T(4,128)} %ids_ref.1, bf16[256,1024]{1,0:T(8,128)(2,1)} %embed_ref.1, bf16[2,1024,4096]{2,1,0:T(8,128)(2,1)} %mix_ref.1, bf16[2,12,4,1024]{3,2,1,0:T(4,128)(2,1)} %fin_raw.1, ...), custom_call_target="tpu_custom_call" | custom-call | tf_op jit(solution)/shard_map/pallas_call | solution.py:557
  81.8 0.0 copy-start
  81.8 1.3 %slice_bitcast_fusion = f32[12,4]{0,1:T(4,128)} fusion(f32[4,128]{1,0:T(4,128)} %get-tuple-element.8), kind=kLoop, calls=%fused_computation.1 | loop fusion | bytes 384 | tf_op jit(solution)/shard_map/transpose | solution.py:614
  83.1 4.9 %convolution_multiply_fusion = f32[2,1024,512]{2,1,0:T(8,128)} fusion(bf16[2,384,1024]{2,1,0:T(8,128)(2,1)} %get-tuple-element.9, bf16[2,384,512]{2,1,0:T(8,128)(2,1)} %get-tuple-element.10), kind=kOutput, calls=%fused_computation | convolution fusion | flops 806354944 | bytes 6553600 | tf_op jit(solution)/shard_map/lki,lko->lio/dot_general | solution.py:615
  88.0 0.0 copy-done
  88.0 0.6 copy.15
Async XLA Ops:
  81.8 6.2 %copy-start = (bf16[12,4,1024]{2,1,0:T(4,128)(2,1)S(1)}, bf16[12,4,1024]{2,1,0:T(4,128)(2,1)}, u32[]{:S(2)}) copy-start(bf16[12,4,1024]{2,1,0:T(4,128)(2,1)} %get-tuple-element.14) | copy-start | bytes 294916
where the time goes:
time: 88.9 us; the launch traced here: 88.7 us
  Pallas kernels  81.2 us (91%)
  matrix products  4.91 us (6%)
  local copies, waits for them, and re-layouts  1.93 us (2%)
    pallas_call x1, Pallas kernels, shards(): pl.pallas_call(functools.partial(policy_kernel, dims), out_shape=(jax.Sha...  81.2 us
    dot_general x1, matrix products, shards(): jnp.einsum('lki,lko->lio', gin, gout, preferred_element_type=f32)  4.91 us

commit v1 on v0

v1 whole, which is shorter than its diff:
```python
import functools

import jax
import jax.numpy as jnp
from jax import lax
from jax.experimental import pallas as pl
from jax.experimental.pallas import tpu as pltpu
from jax.sharding import PartitionSpec as P

noise_scale = 0.25
norm_eps = 1e-06
spread_eps = 1e-05
lanes = 128
f32, bf16 = jnp.float32, jnp.bfloat16


def policy_kernel(
    dims,
    ids_hbm,
    embed_hbm,
    mix_ref,
    fin_hbm,
    fout_hbm,
    ranks_smem,
    decay_hbm,
    gain_hbm,
    reward_hbm,
    final_ref,
    score_ref,
    step_ref,
    ids_ref,
    embed_ref,
    fin_raw,
    fout_raw,
    decay_ref,
    gain_ref,
    reward_ref,
    weights,
    rows_embed,
    own_part,
    got_part,
    own_over,
    got_over,
    mine_part,
    table,
    own_pair,
    got_pair,
    own_cross,
    got_cross,
    states,
    hidden,
    onehot_ref,
    fin_ref,
    fout_ref,
    scaled,
    gin_ref,
    gout_ref,
    granks_ref,
    lows,
    squares,
    leans,
    lasts,
    heads,
    alphas,
    small,
    weight_sem,
    load_sem,
    part_send,
    part_recv,
    over_send,
    over_recv,
    hand_send,
    hand_recv,
    pair_send,
    pair_recv,
    cross_send,
    cross_recv,
    small_send,
    small_recv,
    relay_send,
    relay_recv,
    plane_send,
    plane_recv,
    in_send,
    in_recv,
    pass_send,
    pass_recv,
    out_send,
    out_recv,
    half_send,
    half_recv,
    self_sem,
):
    pop, chunks, group, steps, member_rows, seqs, rank, width, full, coef, share = dims
    parts = pair_send.shape[2]
    piece = width // parts
    halves = [slice(p * piece, (p + 1) * piece) for p in range(parts)]
    rows = group * steps
    vocab = embed_ref.shape[0]
    members = ids_ref.shape[0]
    members_all = members * pop
    layers, local = fin_ref.shape[0], fin_ref.shape[1]
    columns = gout_ref.shape[2]
    mine = lax.axis_index("pop")
    me = lax.axis_index("mp")
    side, core = me // 2, me % 2
    mate = side * 2 + (1 - core)
    cross = (1 - side) * 2 + core
    diagonal = (1 - side) * 2 + (1 - core)
    others = (mate, cross, diagonal)
    blocks = (diagonal, cross, mate, me)
    outer = pop // 2
    line, twin = mine // 2, mine % 2
    buddy = line * 2 + (1 - twin)

    def at_line(place):
        return place * 2 + twin

    def peer(q, j):
        return {"pop": q, "mp": j}

    def remote(src, dst, send, recv, q, j):
        return pltpu.make_async_remote_copy(
            src_ref=src,
            dst_ref=dst,
            send_sem=send,
            recv_sem=recv,
            device_id=peer(q, j),
            device_id_type=pl.DeviceIdType.MESH,
        )

    def weight_copy(layer, slot):
        start = pl.multiple_of(blocks[slot] * width, lanes)
        return pltpu.make_async_copy(
            mix_ref.at[layer, :, pl.ds(start, width)],
            weights.at[slot],
            weight_sem.at[layer, slot],
        )

    loads = [
        pltpu.make_async_copy(src, dst, load_sem.at[i])
        for i, (src, dst) in enumerate(
            (
                (ids_hbm, ids_ref),
                (embed_hbm, embed_ref),
                (fin_hbm, fin_raw),
                (decay_hbm, decay_ref),
                (gain_hbm, gain_ref),
                (reward_hbm, reward_ref),
                (fout_hbm, fout_raw),
            )
        )
    ]
    for copy in loads[:3]:
        copy.start()
    for slot in range(4):
        weight_copy(0, slot).start()
    for copy in loads[3:]:
        copy.start()

    barrier = pltpu.get_barrier_semaphore()

    def greet(q, j):
        pl.semaphore_signal(
            barrier, inc=1, device_id=peer(q, j), device_id_type=pl.DeviceIdType.MESH
        )

    for other in others:
        greet(mine, other)
    greet(buddy, me)

    @pl.when(line < outer - 1)
    def _():
        greet(at_line(line + 1), me)

    @pl.when(line > 0)
    def _():
        greet(at_line(line - 1), me)

    def rank_block(shape, axis, repeats):
        index = lax.broadcasted_iota(jnp.int32, shape, axis)
        block = jnp.zeros(shape, jnp.int32)
        for m in range(members):
            block = jnp.where(index // repeats == m, ranks_smem[m], block)
        return block

    granks_ref[twin, line] = rank_block((8, lanes), 1, 1)

    def unpack(raw, ref):
        def one(g, carry):
            at = pl.ds(
                pl.multiple_of(g * member_rows * rank, member_rows * rank), member_rows * rank
            )
            for layer in range(layers):
                ref[layer, at, :] = jnp.concatenate(
                    [raw[layer, g * member_rows + m].astype(f32) for m in range(member_rows)],
                    axis=0,
                ).astype(bf16)
            return carry

        lax.fori_loop(0, chunks, one, 0)

    factor_rows = member_rows * rank
    mask = (lax.broadcasted_iota(jnp.int32, (factor_rows, rows), 0) // rank) == (
        (lax.broadcasted_iota(jnp.int32, (factor_rows, rows), 1) % group) // seqs
    )

    def factor_slice(ref, layer, g, start, size):
        at = pl.multiple_of(g * factor_rows, factor_rows)
        return ref[layer, pl.ds(at, factor_rows), pl.ds(start, size)]

    def small_copy(kind, g, r):
        return remote(
            small.at[kind, g, 0],
            small.at[kind, g, r + 1],
            small_send.at[kind, g, r],
            small_recv.at[kind, g, r],
            mine,
            others[r],
        )

    def small_start(kind, g):
        for r in range(3):
            small_copy(kind, g, r).start()

    def small_sum(kind, g):
        for r in range(3):
            small_copy(kind, g, r).wait_recv()
        return (small[kind, g, 0] + small[kind, g, 1]) + (small[kind, g, 2] + small[kind, g, 3])

    def against(left, features):
        return lax.dot_general(
            left, features, (((1,), (1,)), ((), ())), preferred_element_type=f32
        )

    def low_put(layer, g, local_low):
        local_low = jnp.where(mask, local_low, 0.0)
        packed = local_low[:rank]
        for at in range(rank, factor_rows, rank):
            packed = packed + local_low[at : at + rank]
        small[layer, g, 0] = packed

    def low_ready(layer, g):
        packed = small_sum(layer, g)
        low = jnp.concatenate([packed] * member_rows, axis=0)
        low = jnp.where(mask, low, 0.0) * coef
        top = low.astype(bf16).astype(f32)
        blank = jnp.zeros((lanes - 2 * factor_rows, rows), f32)
        lows[g] = jnp.concatenate([top, low - top, blank], axis=0).T.astype(bf16)

    def correction(layer, g, p):
        start = pl.multiple_of(me * width + p * piece, lanes)
        factor = factor_slice(fout_ref, layer, g, start, piece)
        right = jnp.concatenate(
            [factor, factor, jnp.zeros((lanes - 2 * factor_rows, piece), bf16)], axis=0
        )
        return jnp.dot(lows[g], right, preferred_element_type=f32)

    loads[0].wait()
    loads[1].wait()
    rows_embed[:share] = embed_ref[pl.ds(pl.multiple_of(twin * share, share), share), :]
    rows_embed[share:] = embed_ref[2 * share :]
    loads[2].wait()
    unpack(fin_raw, fin_ref)

    def begin(g, carry):
        tokens = jnp.concatenate(
            [ids_ref[g * member_rows + m] for m in range(member_rows)], axis=0
        )
        entries = lax.broadcasted_iota(jnp.int32, (group, vocab), 1)
        for t in range(steps):
            onehot_ref[g, t * group : (t + 1) * group, :] = jnp.where(
                tokens[:, t : t + 1] == entries, 1.0, 0.0
            ).astype(bf16)
        features = jnp.dot(onehot_ref[g], embed_ref[...], preferred_element_type=f32).astype(bf16)
        hidden[g] = features
        low_put(0, g, against(factor_slice(fin_ref, 0, g, 0, width), features))
        return carry

    with jax.named_scope("begin"):
        lax.fori_loop(0, chunks, begin, 0)

    def relay_copy(way, hop, source):
        return remote(
            granks_ref.at[twin, source],
            granks_ref.at[twin, source],
            relay_send.at[way, hop],
            relay_recv.at[way, hop],
            at_line(line + 1) if way == 0 else at_line(line - 1),
            me,
        )

    def relay_each(hop, act, sending):
        shift = hop - 1 if sending else hop
        right = (line >= shift) & (line < outer - 1) if sending else line >= shift
        left = (line + shift < outer) & (line > 0) if sending else line + shift < outer

        @pl.when(right)
        def _():
            act(relay_copy(0, hop, line - shift))

        @pl.when(left)
        def _():
            act(relay_copy(1, hop, line + shift))

    def relay_start(hop):
        relay_each(hop, lambda copy: copy.start(), True)

    def relay_next(hop):
        relay_each(hop, lambda copy: copy.wait_recv(), False)
        if hop + 1 < outer:
            relay_start(hop + 1)

    plane = remote(granks_ref.at[twin], granks_ref.at[twin], plane_send, plane_recv, buddy, me)
    plane_in = remote(
        granks_ref.at[1 - twin], granks_ref.at[1 - twin], plane_send, plane_recv, buddy, me
    )

    def part_copy(slot, p):
        return remote(
            own_part.at[slot, p],
            got_part.at[slot, p],
            part_send.at[slot, p],
            part_recv.at[slot, p],
            mine,
            mate,
        )

    spans = (pl.ds(0, share), pl.ds(share, vocab - 2 * share))

    def over_copy(h, p):
        return remote(
            own_over.at[p, spans[h]],
            got_over.at[p, spans[h]],
            over_send.at[h, p],
            over_recv.at[h, p],
            mine,
            cross,
        )

    def hand_copy(p, half):
        at = pl.ds(pl.multiple_of(half * share, share), share)
        return remote(
            table.at[p, at],
            table.at[p, at],
            hand_send.at[p],
            hand_recv.at[p],
            buddy,
            me,
        )

    def entry(slot, p):
        return jnp.dot(
            rows_embed[...], weights[slot, :, halves[p]], preferred_element_type=f32
        ).astype(bf16)

    def part_put(p):
        own_part[0, p] = entry(0, p)

    def part_sum(p):
        value = entry(1, p).astype(f32)
        part_copy(0, p).wait_recv()
        own_over[p] = (value + got_part[0, p].astype(f32)).astype(bf16)
        over_copy(0, p).start()

    early = 2
    with jax.named_scope("tab0"):
        weight_copy(0, 0).wait()
        for p in range(early):
            part_put(p)
    with jax.named_scope("bar"):
        pl.semaphore_wait(
            barrier,
            4 + jnp.where(line < outer - 1, 1, 0) + jnp.where(line > 0, 1, 0),
        )

    relay_start(1)
    for g in range(chunks):
        small_start(0, g)
    with jax.named_scope("tab1"):
        for p in range(early):
            part_copy(0, p).start()
        weight_copy(0, 1).wait()
        for p in range(parts):
            part_sum(p)
            if p + early < parts:
                part_put(p + early)
                part_copy(0, p + early).start()
        for p in range(parts):
            over_copy(1, p).start()
        weight_copy(1, 0).start()
        weight_copy(1, 1).start()
    with jax.named_scope("tab2"):
        weight_copy(0, 2).wait()
        for p in range(parts):
            own_part[1, p] = entry(2, p)
            part_copy(1, p).start()
        weight_copy(1, 2).start()
        weight_copy(0, 3).wait()
        for p in range(parts):
            mine_part[p] = entry(3, p)
        weight_copy(1, 3).start()

    with jax.named_scope("prep"):
        for copy in loads[3:]:
            copy.wait()
        unpack(fout_raw, fout_ref)
        reward = reward_ref[...]
        high = reward.astype(bf16).astype(f32)
        middle = (reward - high).astype(bf16).astype(f32)
        rest = reward - high - middle
        index = lax.broadcasted_iota(jnp.int32, (16, width), 0)
        heads[...] = jnp.where(
            index == 0,
            high,
            jnp.where(index == 1, middle, jnp.where(index == 2, rest, 0.0)),
        ).astype(bf16)
    with jax.named_scope("lowready"):
        for g in range(chunks):
            low_ready(0, g)
    with jax.named_scope("relay1"):
        relay_next(1)

    def both(h, p):
        at = spans[h]
        return (
            mine_part[p, at].astype(f32) + got_part[1, p, at].astype(f32)
        ) + got_over[p, at].astype(f32)

    with jax.named_scope("tabA"):
        for p in range(parts):
            over_copy(0, p).wait_recv()
            part_copy(1, p).wait_recv()
            table[p, pl.ds(pl.multiple_of(twin * share, share), share)] = both(0, p).astype(bf16)
            hand_copy(p, twin).start()
    with jax.named_scope("relay2"):
        if outer > 2:
            relay_next(2)

    def recur(layer, g, p, inputs):
        decay = decay_ref[layer : layer + 1, halves[p]]
        kept = 1.0 - decay
        carried = jnp.zeros((group, piece), f32)
        if layer:
            lean = gain_ref[layer : layer + 1, halves[p]] * reward_ref[:, halves[p]]
        for t in range(steps):
            at = slice(t * group, (t + 1) * group)
            carried = decay * carried + kept * inputs[at]
            if not layer:
                states[g, at, halves[p]] = carried
            elif t == steps - 1:
                lasts[g, :, halves[p]] = carried
            powers = carried * carried
            total = powers[:, :lanes]
            for c in range(lanes, piece, lanes):
                total = total + powers[:, c : c + lanes]
            if p:
                total = total + squares[g, at, :]
            squares[g, at, :] = total
            if layer:
                leaning = carried * lean
                total = leaning[:, :lanes]
                for c in range(lanes, piece, lanes):
                    total = total + leaning[:, c : c + lanes]
                if p:
                    total = total + leans[g, at, :]
                leans[g, at, :] = total

    def across(value):
        return jnp.sum(value.T, axis=0, keepdims=True)

    def squares_start(g):
        small[2, g, 0] = jnp.broadcast_to(across(squares[g]), (4, rows))
        small_start(2, g)

    for p in range(parts):
        with jax.named_scope("tabB%d" % p):
            over_copy(1, p).wait_recv()
            table[p, 2 * share :] = both(1, p).astype(bf16)
        with jax.named_scope("hand%d" % p):
            hand_copy(p, 1 - twin).wait_recv()
        if p == parts - 1:
            with jax.named_scope("relay3"):
                for hop in range(3, outer):
                    relay_next(hop)
                plane.start()
        with jax.named_scope("lz%d" % p):
            for g in range(chunks):
                inputs = jnp.dot(
                    onehot_ref[g], table[p], preferred_element_type=f32
                ) + correction(0, g, p)
                recur(0, g, p, inputs)
                if p == parts - 1:
                    squares_start(g)
    for slot in range(4):
        weight_copy(1, slot).wait()

    def pair_copy(g, slot, p):
        return remote(
            own_pair.at[g, slot, p],
            got_pair.at[g, slot, p],
            pair_send.at[g, slot, p],
            pair_recv.at[g, slot, p],
            mine,
            mate,
        )

    def cross_copy(g, p):
        return remote(
            own_cross.at[g, p],
            got_cross.at[g, p],
            cross_send.at[g, p],
            cross_recv.at[g, p],
            mine,
            cross,
        )

    def own_rows(q):
        return pl.ds(pl.multiple_of(q * local, local), local)

    def in_copy(hop, source):
        return remote(
            scaled,
            gin_ref.at[:, own_rows(at_line(source)), :],
            in_send.at[hop],
            in_recv.at[hop],
            at_line(lax.rem(line + hop, outer)),
            me,
        )

    def in_buddy(source):
        return remote(
            scaled,
            gin_ref.at[:, own_rows(source), :],
            in_send.at[0],
            in_recv.at[0],
            buddy,
            me,
        )

    def pass_copy(hop, side_of):
        at = own_rows(lax.rem(line + outer - hop, outer) * 2 + side_of)
        return remote(
            gin_ref.at[:, at, :],
            gin_ref.at[:, at, :],
            pass_send.at[hop],
            pass_recv.at[hop],
            buddy,
            me,
        )

    def out_copy(hop, source):
        target = lax.rem(mine + hop, pop)
        cols = pl.multiple_of(target * columns, lanes)
        return remote(
            fout_ref.at[core, :, pl.ds(cols, columns)],
            gout_ref.at[core, own_rows(source), :],
            out_send.at[hop],
            out_recv.at[hop],
            target,
            me,
        )

    def half_copy(which):
        return remote(
            gout_ref.at[which],
            gout_ref.at[which],
            half_send,
            half_recv,
            mine,
            mate,
        )

    def self_copies():
        cols = pl.multiple_of(mine * columns, lanes)
        return (
            pltpu.make_async_copy(scaled, gin_ref.at[:, own_rows(mine), :], self_sem.at[0]),
            pltpu.make_async_copy(
                fout_ref.at[core, :, pl.ds(cols, columns)],
                gout_ref.at[core, own_rows(mine), :],
                self_sem.at[1],
            ),
        )

    def shape_ranks():
        full_block = (2, outer, 8, lanes)
        kept = (lax.broadcasted_iota(jnp.int32, full_block, 2) == 0) & (
            lax.broadcasted_iota(jnp.int32, full_block, 3) < members
        )
        shares = jnp.where(kept, granks_ref[...].astype(f32) / members_all, 0.0)

        def mean_of(value):
            value = jnp.sum(value, axis=0)
            value = jnp.sum(value, axis=0)
            value = jnp.sum(value, axis=0, keepdims=True)
            return jnp.sum(value, axis=1, keepdims=True) / members_all

        rank_mean = mean_of(shares)
        apart = jnp.where(kept, shares - rank_mean[None, None], 0.0)
        spread = mean_of(apart * apart) + spread_eps
        own = rank_block((local, lanes), 0, rank).astype(f32) / members_all
        shaped = (own - rank_mean) * lax.rsqrt(spread)
        shaped = jnp.concatenate([shaped] * (width // lanes), axis=1)
        for layer in range(layers):
            scaled[layer] = (fin_ref[layer].astype(f32) * shaped).astype(bf16)

    def gather_start():
        with jax.named_scope("ranks"):
            plane_in.wait_recv()
            shape_ranks()
            in_buddy(mine).start()
            for hop in range(1, outer):
                in_copy(hop, line).start()
            for hop in range(1, pop):
                out_copy(hop, mine).start()
            for copy in self_copies():
                copy.start()

    def gather_pass(first, last):
        with jax.named_scope("pass"):
            for hop in range(first, min(last, outer)):
                in_copy(hop, lax.rem(line + outer - hop, outer)).wait_recv()
                pass_copy(hop, twin).start()

    def gather_half():
        with jax.named_scope("half"):
            for hop in range(1, pop):
                out_copy(hop, lax.rem(mine + pop - hop, pop)).wait_recv()
            for copy in self_copies():
                copy.wait()
            half_copy(core).start()

    def step_make():
        tile = 256
        with jax.named_scope("arrive"):
            in_buddy(buddy).wait_recv()
            for hop in range(1, outer):
                pass_copy(hop, 1 - twin).wait_recv()
            half_copy(1 - core).wait_recv()
        with jax.named_scope("step"):
            for layer in range(layers):
                for at in range(0, width, tile):
                    value = lax.dot_general(
                        gin_ref[layer, :, at : at + tile],
                        gout_ref[layer],
                        (((0,), (0,)), ((), ())),
                        preferred_element_type=f32,
                    )
                    step_ref[layer, at : at + tile] = value * (members_all * rank) ** (-0.5)

    def between(g):
        with jax.named_scope("normed%d" % g):
            total = small_sum(2, g)[:1]
            scale = lax.rsqrt(total / full + norm_eps)
            scale = jnp.broadcast_to(scale, (lanes, rows)).T
            scale = jnp.concatenate([scale] * (width // lanes), axis=1)
            gain = gain_ref[0:1, :]
            hidden[g] = (hidden[g].astype(f32) + states[g] * scale * gain).astype(bf16)

        def product(slot, p):
            return jnp.dot(
                hidden[g], weights[slot, :, halves[p]], preferred_element_type=f32
            ).astype(bf16)

        with jax.named_scope("exch%d" % g):
            def summed(p):
                value = product(1, p).astype(f32)
                pair_copy(g, 0, p).wait_recv()
                own_cross[g, p] = (value + got_pair[g, 0, p].astype(f32)).astype(bf16)
                cross_copy(g, p).start()

            for p in range(parts):
                own_pair[g, 0, p] = product(0, p)
                pair_copy(g, 0, p).start()
                if p:
                    summed(p - 1)
            left = jnp.concatenate([factor_slice(fin_ref, 1, g, 0, width), heads[...]], axis=0)
            local_low = against(left, hidden[g])
            low_put(1, g, local_low[:factor_rows])
            small_start(1, g)
            aligned = local_low[factor_rows : factor_rows + 8]
            alphas[g] = jnp.broadcast_to(jnp.sum(aligned, axis=0, keepdims=True), (8, rows))
            summed(parts - 1)
            if g == 0:
                gather_start()
            for p in range(parts):
                own_pair[g, 1, p] = product(2, p)
                pair_copy(g, 1, p).start()
            for p in range(parts):
                states[g, :, halves[p]] = product(3, p).astype(f32)

    def layer_one(g):
        with jax.named_scope("lowone%d" % g):
            low_ready(1, g)
        for p in range(parts):
            with jax.named_scope("l1_%d_%d" % (g, p)):
                pair_copy(g, 1, p).wait_recv()
                fixed = (
                    states[g, :, halves[p]] + got_pair[g, 1, p].astype(f32)
                ) + correction(1, g, p)
                cross_copy(g, p).wait_recv()
                recur(1, g, p, fixed + got_cross[g, p].astype(f32))
        with jax.named_scope("end%d" % g):
            small[3, g, 0] = jnp.concatenate(
                [across(squares[g]), across(leans[g]), alphas[g][:2]], axis=0
            )
            small_start(3, g)

    for g in range(chunks):
        between(g)
        if g:
            gather_pass(g, g + 1)
    for g in range(chunks):
        if g == chunks - 1:
            gather_pass(chunks, outer)
            gather_half()
            if g:
                layer_one(g - 1)
            step_make()
            layer_one(g)
        elif g < chunks - 2:
            layer_one(g)

    lane = lax.broadcasted_iota(jnp.int32, (seqs, lanes), 1)
    scores = jnp.zeros((seqs, lanes), f32)
    with jax.named_scope("final"):
        for g in range(chunks):
            sums = small_sum(3, g)
            scale = lax.rsqrt(sums[0:1] / full + norm_eps)
            value = sums[2:3] + scale * sums[1:2]
            total = value[:, :lanes]
            for c in range(lanes, rows, lanes):
                total = total + value[:, c : c + lanes]
            total = jnp.broadcast_to(total, (8, lanes))
            shift = lanes // 2
            while shift >= group:
                total = total + pltpu.roll(total, shift, 1)
                shift //= 2
            total = total * (full ** (-0.5) / steps)
            total = jnp.broadcast_to(total[:1], (lanes, lanes)).T
            for m in range(member_rows):
                scores = jnp.where(
                    lane == g * member_rows + m, total[m * seqs : (m + 1) * seqs], scores
                )
            ending = jnp.broadcast_to(scale[:, rows - lanes :], (lanes, lanes)).T[lanes - group :]
            ending = jnp.concatenate([ending] * (width // lanes), axis=1)
            gain = gain_ref[1:2, :]
            ending = (
                hidden[g, rows - group :].astype(f32) + lasts[g] * ending * gain
            ).astype(bf16).astype(f32)
            for m in range(member_rows):
                final_ref[g * member_rows + m] = ending[m * seqs : (m + 1) * seqs].astype(bf16)
        score_ref[...] = scores

    with jax.named_scope("drain"):
        for hop in range(1, outer):
            relay_each(hop, lambda copy: copy.wait_send(), True)
        plane.wait_send()
        for p in range(parts):
            for slot in range(2):
                part_copy(slot, p).wait_send()
                over_copy(slot, p).wait_send()
            hand_copy(p, twin).wait_send()
        for g in range(chunks):
            for p in range(parts):
                pair_copy(g, 0, p).wait_send()
                pair_copy(g, 1, p).wait_send()
                cross_copy(g, p).wait_send()
            for kind in range(4):
                for r in range(3):
                    small_copy(kind, g, r).wait_send()
        in_buddy(mine).wait_send()
        for hop in range(1, outer):
            in_copy(hop, line).wait_send()
            pass_copy(hop, twin).wait_send()
        for hop in range(1, pop):
            out_copy(hop, mine).wait_send()
        half_copy(core).wait_send()


cuts = 4


def publish(final_ref, marks_ref, step_ref, final_out, score_out, step_out, sems):
    copies = [pltpu.make_async_copy(final_ref, final_out, sems.at[2, 0])]
    layers, width, _ = step_ref.shape
    cut = width // cuts
    for layer in range(layers):
        for c in range(cuts):
            at = pl.ds(c * cut, cut)
            copies.append(
                pltpu.make_async_copy(
                    step_ref.at[layer, at], step_out.at[layer, at], sems.at[layer, c]
                )
            )
    for copy in copies:
        copy.start()
    score_out[...] = marks_ref[:, : score_out.shape[1]]
    for copy in copies:
        copy.wait()


def shards(
    token_ids,
    fitness_ranks,
    embedding,
    mix_weights,
    factors_in,
    factors_out,
    decay_rates,
    norm_gain,
    reward_dir,
):
    members, seqs, steps = token_ids.shape
    vocab, width = embedding.shape
    layers, _, full = mix_weights.shape
    rank = factors_in.shape[2]
    pop = lax.axis_size("pop")
    outer = pop // 2
    coef = noise_scale * (full * rank) ** (-0.5)
    columns = full // pop
    member_rows = 16 // seqs
    chunks = members // member_rows
    group = member_rows * seqs
    rows = group * steps
    local = members * rank
    share = vocab * 3 // 8
    dims = (pop, chunks, group, steps, member_rows, seqs, rank, width, full, coef, share)
    vmem = pl.BlockSpec(memory_space=pltpu.VMEM)
    smem = pl.BlockSpec(memory_space=pltpu.SMEM)
    hbm = pl.BlockSpec(memory_space=pltpu.HBM)
    parts = 4
    piece = width // parts
    entries = vocab - share
    dma = pltpu.SemaphoreType.DMA
    final_features, marks, step = pl.pallas_call(
        functools.partial(policy_kernel, dims),
        out_shape=(
            pltpu.VMEM((members, seqs, width), bf16),
            pltpu.VMEM((seqs, lanes), f32),
            pltpu.VMEM((layers, width, columns), f32),
        ),
        in_specs=[hbm, hbm, hbm, hbm, hbm, smem, hbm, hbm, hbm],
        out_specs=(vmem, vmem, vmem),
        scratch_shapes=[
            pltpu.VMEM((members, seqs, steps), jnp.int32),
            pltpu.VMEM((vocab, width), bf16),
            pltpu.VMEM((layers, members, rank, width), bf16),
            pltpu.VMEM((layers, members, rank, full), bf16),
            pltpu.VMEM((layers, width), f32),
            pltpu.VMEM((layers, width), f32),
            pltpu.VMEM((1, width), f32),
            pltpu.VMEM((4, width, width), bf16),
            pltpu.VMEM((entries, width), bf16),
            pltpu.VMEM((2, parts, entries, piece), bf16),
            pltpu.VMEM((2, parts, entries, piece), bf16),
            pltpu.VMEM((parts, entries, piece), bf16),
            pltpu.VMEM((parts, entries, piece), bf16),
            pltpu.VMEM((parts, entries, piece), bf16),
            pltpu.VMEM((parts, vocab, piece), bf16),
            pltpu.VMEM((chunks, 2, parts, rows, piece), bf16),
            pltpu.VMEM((chunks, 2, parts, rows, piece), bf16),
            pltpu.VMEM((chunks, parts, rows, piece), bf16),
            pltpu.VMEM((chunks, parts, rows, piece), bf16),
            pltpu.VMEM((chunks, rows, width), f32),
            pltpu.VMEM((chunks, rows, width), bf16),
            pltpu.VMEM((chunks, rows, vocab), bf16),
            pltpu.VMEM((layers, local, width), bf16),
            pltpu.VMEM((layers, local, full), bf16),
            pltpu.VMEM((layers, local, width), bf16),
            pltpu.VMEM((layers, pop * local, width), bf16),
            pltpu.VMEM((layers, pop * local, columns), bf16),
            pltpu.VMEM((2, outer, 8, lanes), jnp.int32),
            pltpu.VMEM((chunks, rows, lanes), bf16),
            pltpu.VMEM((chunks, rows, lanes), f32),
            pltpu.VMEM((chunks, rows, lanes), f32),
            pltpu.VMEM((chunks, group, width), f32),
            pltpu.VMEM((16, width), bf16),
            pltpu.VMEM((chunks, 8, rows), f32),
            pltpu.VMEM((4, chunks, 4, 4, rows), f32),
            dma((layers, 4)),
            dma((7,)),
            dma((2, parts)),
            dma((2, parts)),
            dma((2, parts)),
            dma((2, parts)),
            dma((parts,)),
            dma((parts,)),
            dma((chunks, 2, parts)),
            dma((chunks, 2, parts)),
            dma((chunks, parts)),
            dma((chunks, parts)),
            dma((4, chunks, 3)),
            dma((4, chunks, 3)),
            dma((2, outer)),
            dma((2, outer)),
            dma,
            dma,
            dma((outer,)),
            dma((outer,)),
            dma((outer,)),
            dma((outer,)),
            dma((pop,)),
            dma((pop,)),
            dma,
            dma,
            dma((2,)),
        ],
        compiler_params=pltpu.CompilerParams(
            collective_id=0, has_side_effects=True, vmem_limit_bytes=52 * 1024 * 1024
        ),
    )(
        *(
            pltpu.with_memory_space_constraint(value, pltpu.HBM)
            for value in (
                token_ids,
                embedding,
                mix_weights,
                factors_in,
                factors_out,
                fitness_ranks,
                decay_rates,
                norm_gain,
                reward_dir.reshape(1, width),
            )
        )
    )
    final_features, scores, weight_step = pl.pallas_call(
        publish,
        out_shape=(
            jax.ShapeDtypeStruct((members, seqs, width), bf16),
            jax.ShapeDtypeStruct((seqs, members), f32),
            jax.ShapeDtypeStruct((layers, width, columns), f32),
        ),
        in_specs=[vmem, vmem, vmem],
        out_specs=(hbm, vmem, hbm),
        scratch_shapes=[dma((3, cuts))],
        compiler_params=pltpu.CompilerParams(vmem_limit_bytes=1024 * 1024),
    )(final_features, marks, step)
    return (final_features, scores.T, weight_step)


def solution(mesh):
    return jax.shard_map(
        shards,
        mesh=mesh,
        in_specs=(
            P("pop", None, None),
            P("pop"),
            P(None, "mp"),
            P(None, "mp", None),
            P(None, "pop", None, "mp"),
            P(None, "pop", None, None),
            P(None, "mp"),
            P(None, "mp"),
            P("mp"),
        ),
        out_specs=(P("pop", None, "mp"), P("pop", None), P(None, "mp", "pop")),
        check_vma=False,
    )
```

time: 88.9 us -> 68.5 us (0.77)
  Pallas kernels: 81.2 us -> 67.4 us
  matrix products: 4.91 us -> 0 us
  local copies, waits for them, and re-layouts: 1.93 us -> 0 us
    pallas_call x1 -> x2, Pallas kernels: 81.2 us -> 67.4 us  [the longest x1 64.6 us: shards(): pl.pallas_call(functools.partial(policy_kernel, dims), out_shape=(pltpu.V...]
    dot_general x1 -> x0, matrix products: 4.91 us -> none  [shards(): jnp.einsum('lki,lko->lio', gin, gout, preferred_element_type=f32)]
    transpose x1 -> x0, local copies, waits for them, and re-layouts: 1.28 us -> none  [shards(): scores = marks[:, :members].T]
where the time goes in v1:
time: 68.5 us; the launch traced here: 68.2 us
  Pallas kernels  67.4 us (98%)
  between operations  0.8 us (1%)
    pallas_call x1, Pallas kernels, shards(): pl.pallas_call(functools.partial(policy_kernel, dims), out_shape=(pltpu.V...  64.6 us
    pallas_call x1, Pallas kernels, shards(): pl.pallas_call(publish, out_shape=(jax.ShapeDtypeStruct((members, seqs, w...  2.72 us

profile of v1, /device:TPU:0, one launch (start us, length us, event | category | flops | bytes accessed | tf_op | source)
XLA Modules:
  0.0 68.2 jit_solution(15441098595243630185)
XLA Ops:
  0.6 64.6 %shard_map.112 = (bf16[12,4,1024]{2,1,0:T(4,128)(2,1)S(1)}, f32[4,128]{1,0:T(4,128)S(1)}, f32[2,1024,512]{2,1,0:T(8,128)S(1)}) custom-call(s32[12,4,16]{2,1,0:T(4,128)} %ids_hbm.1, bf16[256,1024]{1,0:T(8,128)(2,1)} %embed_hbm.1, bf16[2,1024,4096]{2,1,0:T(8,128)(2,1)} %mix_ref.1, bf16[2,12,4,1024]{3,2,1,0:T(4,128)(2,1)} %fin_hbm.1, ...), custom_call_target="tpu_custom_call" | custom-call | tf_op jit(solution)/shard_map/pallas_call | solution.py:836
  65.3 2.7 %shard_map.113 = (bf16[12,4,1024]{2,1,0:T(4,128)(2,1)}, f32[4,12]{1,0:T(4,128)}, f32[2,1024,512]{2,1,0:T(8,128)}) custom-call(bf16[12,4,1024]{2,1,0:T(4,128)(2,1)S(1)} %get-tuple-element.9.final_ref, f32[4,128]{1,0:T(4,128)S(1)} %get-tuple-element.10.marks_ref, f32[2,1024,512]{2,1,0:T(8,128)S(1)} %get-tuple-element.11.step_ref), custom_call_target="tpu_custom_call" | custom-call | tf_op jit(solution)/shard_map/pallas_call | solution.py:928

commit v2 on v1

--- a/solution.py
+++ b/solution.py
@@ -47,6 +47,12 @@
     got_pair,
     own_cross,
     got_cross,
+    own_lead,
+    got_lead,
+    own_ahead,
+    got_ahead,
+    lifted,
+    lead_scale,
     states,
     hidden,
     onehot_ref,
@@ -64,6 +70,7 @@
     alphas,
     small,
     weight_sem,
+    column_sem,
     load_sem,
     part_send,
     part_recv,
@@ -75,6 +82,10 @@
     pair_recv,
     cross_send,
     cross_recv,
+    lead_send,
+    lead_recv,
+    ahead_send,
+    ahead_recv,
     small_send,
     small_recv,
     relay_send,
@@ -92,7 +103,7 @@
     self_sem,
 ):
     pop, chunks, group, steps, member_rows, seqs, rank, width, full, coef, share = dims
-    parts = pair_send.shape[2]
+    parts = cross_recv.shape[1]
     piece = width // parts
     halves = [slice(p * piece, (p + 1) * piece) for p in range(parts)]
     rows = group * steps
@@ -129,20 +140,47 @@
             device_id_type=pl.DeviceIdType.MESH,
         )
 
+    barrier = pltpu.get_barrier_semaphore()
+
+    def greet(q, j):
+        pl.semaphore_signal(
+            barrier, inc=1, device_id=peer(q, j), device_id_type=pl.DeviceIdType.MESH
+        )
+
+    for other in others:
+        greet(mine, other)
+    greet(buddy, me)
+
+    @pl.when(line < outer - 1)
+    def _():
+        greet(at_line(line + 1), me)
+
+    @pl.when(line > 0)
+    def _():
+        greet(at_line(line - 1), me)
+
     def weight_copy(layer, slot):
         start = pl.multiple_of(blocks[slot] * width, lanes)
         return pltpu.make_async_copy(
             mix_ref.at[layer, :, pl.ds(start, width)],
             weights.at[slot],
-            weight_sem.at[layer, slot],
+            weight_sem.at[2 if layer else slot - 2],
+        )
+
+    def column_copy(slot, p):
+        start = pl.multiple_of(blocks[slot] * width + p * piece, lanes)
+        return pltpu.make_async_copy(
+            mix_ref.at[0, :, pl.ds(start, piece)],
+            weights.at[slot, :, halves[p]],
+            column_sem.at[slot, p],
         )
 
     loads = [
         pltpu.make_async_copy(src, dst, load_sem.at[i])
         for i, (src, dst) in enumerate(
             (
+                (embed_hbm, embed_ref),
                 (ids_hbm, ids_ref),
-                (embed_hbm, embed_ref),
                 (fin_hbm, fin_raw),
                 (decay_hbm, decay_ref),
                 (gain_hbm, gain_ref),
@@ -151,31 +189,16 @@
             )
         )
     ]
-    for copy in loads[:3]:
+    loads[0].start()
+    for slot in range(2):
+        for p in range(parts):
+            column_copy(slot, p).start()
+    for copy in loads[1:3]:
         copy.start()
-    for slot in range(4):
-        weight_copy(0, slot).start()
+    weight_copy(0, 2).start()
+    weight_copy(0, 3).start()
     for copy in loads[3:]:
         copy.start()
-
-    barrier = pltpu.get_barrier_semaphore()
-
-    def greet(q, j):
-        pl.semaphore_signal(
-            barrier, inc=1, device_id=peer(q, j), device_id_type=pl.DeviceIdType.MESH
-        )
-
-    for other in others:
-        greet(mine, other)
-    greet(buddy, me)
-
-    @pl.when(line < outer - 1)
-    def _():
-        greet(at_line(line + 1), me)
-
-    @pl.when(line > 0)
-    def _():
-        greet(at_line(line - 1), me)
 
     def rank_block(shape, axis, repeats):
         index = lax.broadcasted_iota(jnp.int32, shape, axis)
@@ -213,8 +236,8 @@
         return remote(
             small.at[kind, g, 0],
             small.at[kind, g, r + 1],
-            small_send.at[kind, g, r],
-            small_recv.at[kind, g, r],
+            small_send,
+            small_recv.at[kind, g],
             mine,
             others[r],
         )
@@ -224,8 +247,8 @@
             small_copy(kind, g, r).start()
 
     def small_sum(kind, g):
-        for r in range(3):
-            small_copy(kind, g, r).wait_recv()
+        arrived = small.at[kind, g, pl.ds(1, 3)]
+        remote(arrived, arrived, small_send, small_recv.at[kind, g], mine, mate).wait_recv()
         return (small[kind, g, 0] + small[kind, g, 1]) + (small[kind, g, 2] + small[kind, g, 3])
 
     def against(left, features):
@@ -257,9 +280,120 @@
         return jnp.dot(lows[g], right, preferred_element_type=f32)
 
     loads[0].wait()
-    loads[1].wait()
     rows_embed[:share] = embed_ref[pl.ds(pl.multiple_of(twin * share, share), share), :]
     rows_embed[share:] = embed_ref[2 * share :]
+    def relay_copy(way, hop, source):
+        return remote(
+            granks_ref.at[twin, source],
+            granks_ref.at[twin, source],
+            relay_send.at[way, hop - 1],
+            relay_recv.at[way, hop - 1],
+            at_line(line + 1) if way == 0 else at_line(line - 1),
+            me,
+        )
+
+    def relay_each(hop, act, sending):
+        shift = hop - 1 if sending else hop
+        right = (line >= shift) & (line < outer - 1) if sending else line >= shift
+        left = (line + shift < outer) & (line > 0) if sending else line + shift < outer
+
+        @pl.when(right)
+        def _():
+            act(relay_copy(0, hop, line - shift))
+
+        @pl.when(left)
+        def _():
+            act(relay_copy(1, hop, line + shift))
+
+    def relay_start(hop):
+        relay_each(hop, lambda copy: copy.start(), True)
+
+    def relay_next(hop):
+        relay_each(hop, lambda copy: copy.wait_recv(), False)
+        if hop + 1 < outer:
+            relay_start(hop + 1)
+
+    plane = remote(granks_ref.at[twin], granks_ref.at[twin], plane_send, plane_recv, buddy, me)
+    plane_in = remote(
+        granks_ref.at[1 - twin], granks_ref.at[1 - twin], plane_send, plane_recv, buddy, me
+    )
+
+    def part_copy(slot, p):
+        return remote(
+            own_part.at[slot, p],
+            got_part.at[slot, p],
+            part_send,
+            part_recv.at[parts if slot else p],
+            mine,
+            mate,
+        )
+
+    def whole_part(slot):
+        return remote(
+            own_part.at[slot], got_part.at[slot], part_send, part_recv.at[parts], mine, mate
+        )
+
+    spans = (pl.ds(0, share), pl.ds(share, vocab - 2 * share))
+
+    def over_copy(h, p):
+        return remote(
+            own_over.at[p, spans[h]],
+            got_over.at[p, spans[h]],
+            over_send,
+            over_recv.at[h, p],
+            mine,
+            cross,
+        )
+
+    def hand_copy(p, half):
+        at = pl.ds(pl.multiple_of(half * share, share), share)
+        return remote(
+            table.at[p, at],
+            table.at[p, at],
+            hand_send,
+            hand_recv.at[p],
+            buddy,
+            me,
+        )
+
+    def entry(slot, p):
+        return jnp.dot(
+            rows_embed[...], weights[slot, :, halves[p]], preferred_element_type=f32
+        ).astype(bf16)
+
+    def part_put(p):
+        column_copy(0, p).wait()
+        own_part[0, p] = entry(0, p)
+
+    def part_sum(p):
+        column_copy(1, p).wait()
+        value = entry(1, p).astype(f32)
+        part_copy(0, p).wait_recv()
+        own_over[p] = (value + got_part[0, p].astype(f32)).astype(bf16)
+        over_copy(0, p).start()
+
+    early = 2
+    with jax.named_scope("tab0"):
+        for p in range(early):
+            part_put(p)
+    with jax.named_scope("bar"):
+        pl.semaphore_wait(
+            barrier,
+            4 + jnp.where(line < outer - 1, 1, 0) + jnp.where(line > 0, 1, 0),
+        )
+
+    relay_start(1)
+    with jax.named_scope("tab1"):
+        for p in range(early):
+            part_copy(0, p).start()
+        for p in range(early, parts):
+            part_put(p)
+            part_copy(0, p).start()
+        for p in range(parts):
+            part_sum(p)
+        weight_copy(1, 0).start()
+        weight_copy(1, 1).start()
+    loads[1].wait()
     loads[2].wait()
     unpack(fin_raw, fin_ref)
 
@@ -280,116 +414,12 @@
     with jax.named_scope("begin"):
         lax.fori_loop(0, chunks, begin, 0)
 
-    def relay_copy(way, hop, source):
-        return remote(
-            granks_ref.at[twin, source],
-            granks_ref.at[twin, source],
-            relay_send.at[way, hop],
-            relay_recv.at[way, hop],
-            at_line(line + 1) if way == 0 else at_line(line - 1),
-            me,
-        )
-
-    def relay_each(hop, act, sending):
-        shift = hop - 1 if sending else hop
-        right = (line >= shift) & (line < outer - 1) if sending else line >= shift
-        left = (line + shift < outer) & (line > 0) if sending else line + shift < outer
-
-        @pl.when(right)
-        def _():
-            act(relay_copy(0, hop, line - shift))
-
-        @pl.when(left)
-        def _():
-            act(relay_copy(1, hop, line + shift))
-
-    def relay_start(hop):
-        relay_each(hop, lambda copy: copy.start(), True)
-
-    def relay_next(hop):
-        relay_each(hop, lambda copy: copy.wait_recv(), False)
-        if hop + 1 < outer:
-            relay_start(hop + 1)
-
-    plane = remote(granks_ref.at[twin], granks_ref.at[twin], plane_send, plane_recv, buddy, me)
-    plane_in = remote(
-        granks_ref.at[1 - twin], granks_ref.at[1 - twin], plane_send, plane_recv, buddy, me
-    )
-
-    def part_copy(slot, p):
-        return remote(
-            own_part.at[slot, p],
-            got_part.at[slot, p],
-            part_send.at[slot, p],
-            part_recv.at[slot, p],
-            mine,
-            mate,
-        )
-
-    spans = (pl.ds(0, share), pl.ds(share, vocab - 2 * share))
-
-    def over_copy(h, p):
-        return remote(
-            own_over.at[p, spans[h]],
-            got_over.at[p, spans[h]],
-            over_send.at[h, p],
-            over_recv.at[h, p],
-            mine,
-            cross,
-        )
-
-    def hand_copy(p, half):
-        at = pl.ds(pl.multiple_of(half * share, share), share)
-        return remote(
-            table.at[p, at],
-            table.at[p, at],
-            hand_send.at[p],
-            hand_recv.at[p],
-            buddy,
-            me,
-        )
-
-    def entry(slot, p):
-        return jnp.dot(
-            rows_embed[...], weights[slot, :, halves[p]], preferred_element_type=f32
-        ).astype(bf16)
-
-    def part_put(p):
-        own_part[0, p] = entry(0, p)
-
-    def part_sum(p):
-        value = entry(1, p).astype(f32)
-        part_copy(0, p).wait_recv()
-        own_over[p] = (value + got_part[0, p].astype(f32)).astype(bf16)
-        over_copy(0, p).start()
-
-    early = 2
-    with jax.named_scope("tab0"):
-        weight_copy(0, 0).wait()
-        for p in range(early):
-            part_put(p)
-    with jax.named_scope("bar"):
-        pl.semaphore_wait(
-            barrier,
-            4 + jnp.where(line < outer - 1, 1, 0) + jnp.where(line > 0, 1, 0),
-        )
-
-    relay_start(1)
     for g in range(chunks):
         small_start(0, g)
-    with jax.named_scope("tab1"):
-        for p in range(early):
-            part_copy(0, p).start()
-        weight_copy(0, 1).wait()
-        for p in range(parts):
-            part_sum(p)
-            if p + early < parts:
-                part_put(p + early)
-                part_copy(0, p + early).start()
-        for p in range(parts):
-            over_copy(1, p).start()
-        weight_copy(1, 0).start()
-        weight_copy(1, 1).start()
+    for p in range(parts):
+        over_copy(1, p).start()
+    with jax.named_scope("relay1"):
+        relay_next(1)
     with jax.named_scope("tab2"):
         weight_copy(0, 2).wait()
         for p in range(parts):
@@ -415,11 +445,6 @@
             high,
             jnp.where(index == 1, middle, jnp.where(index == 2, rest, 0.0)),
         ).astype(bf16)
-    with jax.named_scope("lowready"):
-        for g in range(chunks):
-            low_ready(0, g)
-    with jax.named_scope("relay1"):
-        relay_next(1)
 
     def both(h, p):
         at = spans[h]
@@ -427,15 +452,64 @@
             mine_part[p, at].astype(f32) + got_part[1, p, at].astype(f32)
         ) + got_over[p, at].astype(f32)
 
+    lead = lifted.shape[0]
+
+    def lead_pair(k, p):
+        return remote(
+            own_lead.at[k, p],
+            got_lead.at[k, p],
+            lead_send,
+            lead_recv.at[1 + p if k else 0],
+            mine,
+            mate,
+        )
+
+    def whole_lead():
+        return remote(own_lead.at[0], got_lead.at[0], lead_send, lead_recv.at[0], mine, mate)
+
+    def lead_cross(k, p):
+        return remote(
+            own_ahead.at[k, p], got_ahead.at[k, p], ahead_send, ahead_recv, mine, cross
+        )
+
+    def lead_rows(k):
+        return lifted[...] if k else hidden[0, :lead]
+
+    def lead_put(k, p):
+        if k == 0 and p == 0:
+            wait_weights()
+        own_lead[k, p] = jnp.dot(
+            lead_rows(k), weights[0, :, halves[p]], preferred_element_type=f32
+        ).astype(bf16)
+        lead_pair(k, p).start()
+
+    def lead_sum(k, p):
+        value = (
+            jnp.dot(lead_rows(k), weights[1, :, halves[p]], preferred_element_type=f32)
+            .astype(bf16)
+            .astype(f32)
+        )
+        if k:
+            lead_pair(k, p).wait_recv()
+        own_ahead[k, p] = (value + got_lead[k, p].astype(f32)).astype(bf16)
+        lead_cross(k, p).start()
+
+    def wait_weights():
+        pltpu.make_async_copy(weights, weights, weight_sem.at[2]).wait()
+
     with jax.named_scope("tabA"):
         for p in range(parts):
             over_copy(0, p).wait_recv()
-            part_copy(1, p).wait_recv()
+            if p == 0:
+                whole_part(1).wait_recv()
             table[p, pl.ds(pl.multiple_of(twin * share, share), share)] = both(0, p).astype(bf16)
             hand_copy(p, twin).start()
-    with jax.named_scope("relay2"):
-        if outer > 2:
-            relay_next(2)
+            lead_put(0, p)
+            if p == 1 and outer > 2:
+                relay_next(2)
+    with jax.named_scope("lowready"):
+        for g in range(chunks):
+            low_ready(0, g)
 
     def recur(layer, g, p, inputs):
         decay = decay_ref[layer : layer + 1, halves[p]]
@@ -477,9 +551,13 @@
         with jax.named_scope("tabB%d" % p):
             over_copy(1, p).wait_recv()
             table[p, 2 * share :] = both(1, p).astype(bf16)
+        with jax.named_scope("lead%d" % p):
+            if p == 0:
+                whole_lead().wait_recv()
+            lead_sum(0, p)
         with jax.named_scope("hand%d" % p):
             hand_copy(p, 1 - twin).wait_recv()
-        if p == parts - 1:
+        if p == 0:
             with jax.named_scope("relay3"):
                 for hop in range(3, outer):
                     relay_next(hop)
@@ -492,24 +570,35 @@
                 recur(0, g, p, inputs)
                 if p == parts - 1:
                     squares_start(g)
-    for slot in range(4):
-        weight_copy(1, slot).wait()
-
+                    if g == 0:
+                        with jax.named_scope("leadv"):
+                            lift = states[0, :lead] * gain_ref[0:1, :]
+                            lifted[...] = lift.astype(bf16)
+                            for q in range(parts):
+                                lead_put(1, q)
+                            for q in range(parts):
+                                lead_sum(1, q)
     def pair_copy(g, slot, p):
         return remote(
             own_pair.at[g, slot, p],
             got_pair.at[g, slot, p],
-            pair_send.at[g, slot, p],
-            pair_recv.at[g, slot, p],
+            pair_send,
+            pair_recv.at[g, parts if slot else p],
             mine,
             mate,
         )
 
+    def whole_pair(g):
+        return remote(
+            own_pair.at[g, 1], got_pair.at[g, 1], pair_send, pair_recv.at[g, parts], mine, mate
+        )
+
     def cross_copy(g, p):
-        return remote(
-            own_cross.at[g, p],
-            got_cross.at[g, p],
-            cross_send.at[g, p],
+        at = pl.ds(0 if g else lead, rows if g else rows - lead)
+        return remote(
+            own_cross.at[g, p, at],
+            got_cross.at[g, p, at],
+            cross_send.at[1 if g else 0],
             cross_recv.at[g, p],
             mine,
             cross,
@@ -522,7 +611,7 @@
         return remote(
             scaled,
             gin_ref.at[:, own_rows(at_line(source)), :],
-            in_send.at[hop],
+            in_send,
             in_recv.at[hop],
             at_line(lax.rem(line + hop, outer)),
             me,
@@ -532,7 +621,7 @@
         return remote(
             scaled,
             gin_ref.at[:, own_rows(source), :],
-            in_send.at[0],
+            in_send,
             in_recv.at[0],
             buddy,
             me,
@@ -543,8 +632,8 @@
         return remote(
             gin_ref.at[:, at, :],
             gin_ref.at[:, at, :],
-            pass_send.at[hop],
-            pass_recv.at[hop],
+            pass_send,
+            pass_recv,
             buddy,
             me,
         )
@@ -555,11 +644,26 @@
         return remote(
             fout_ref.at[core, :, pl.ds(cols, columns)],
             gout_ref.at[core, own_rows(source), :],
-            out_send.at[hop],
-            out_recv.at[hop],
+            out_send,
+            out_recv,
             target,
             me,
         )
+
+    def stretch(ref, count):
+        return ref.at[pl.ds(0, count * local), :]
+
+    def whole_out():
+        spot = stretch(gout_ref.at[core], pop - 1)
+        return remote(spot, spot, out_send, out_recv, buddy, me)
+
+    def whole_pass():
+        spot = gin_ref.at[:, pl.ds(0, (outer - 1) * local), :]
+        return remote(spot, spot, pass_send, pass_recv, buddy, me)
+
+    def whole_in():
+        spot = gin_ref.at[:, pl.ds(0, outer * local), :]
+        return remote(spot, spot, in_send, in_recv.at[0], buddy, me)
 
     def half_copy(which):
         return remote(
@@ -624,8 +728,7 @@
 
     def gather_half():
         with jax.named_scope("half"):
-            for hop in range(1, pop):
-                out_copy(hop, lax.rem(mine + pop - hop, pop)).wait_recv()
+            whole_out().wait_recv()
             for copy in self_copies():
                 copy.wait()
             half_copy(core).start()
@@ -634,8 +737,9 @@
         tile = 256
         with jax.named_scope("arrive"):
             in_buddy(buddy).wait_recv()
-            for hop in range(1, outer):
-                pass_copy(hop, 1 - twin).wait_recv()
+        with jax.named_scope("arrive_pass"):
+            whole_pass().wait_recv()
+        with jax.named_scope("arrive_half"):
             half_copy(1 - core).wait_recv()
         with jax.named_scope("step"):
             for layer in range(layers):
@@ -653,6 +757,8 @@
             total = small_sum(2, g)[:1]
             scale = lax.rsqrt(total / full + norm_eps)
             scale = jnp.broadcast_to(scale, (lanes, rows)).T
+            if g == 0:
+                lead_scale[...] = scale[:lead]
             scale = jnp.concatenate([scale] * (width // lanes), axis=1)
             gain = gain_ref[0:1, :]
             hidden[g] = (hidden[g].astype(f32) + states[g] * scale * gain).astype(bf16)
@@ -666,7 +772,11 @@
             def summed(p):
                 value = product(1, p).astype(f32)
                 pair_copy(g, 0, p).wait_recv()
-                own_cross[g, p] = (value + got_pair[g, 0, p].astype(f32)).astype(bf16)
+                total = (value + got_pair[g, 0, p].astype(f32)).astype(bf16)
+                if g:
+                    own_cross[g, p] = total
+                else:
+                    own_cross[g, p, lead:] = total[lead:]
                 cross_copy(g, p).start()
 
             for p in range(parts):
@@ -681,8 +791,6 @@
             aligned = local_low[factor_rows : factor_rows + 8]
             alphas[g] = jnp.broadcast_to(jnp.sum(aligned, axis=0, keepdims=True), (8, rows))
             summed(parts - 1)
-            if g == 0:
-                gather_start()
             for p in range(parts):
                 own_pair[g, 1, p] = product(2, p)
                 pair_copy(g, 1, p).start()
@@ -694,18 +802,30 @@
             low_ready(1, g)
         for p in range(parts):
             with jax.named_scope("l1_%d_%d" % (g, p)):
-                pair_copy(g, 1, p).wait_recv()
+                if p == 0:
+                    whole_pair(g).wait_recv()
                 fixed = (
                     states[g, :, halves[p]] + got_pair[g, 1, p].astype(f32)
                 ) + correction(1, g, p)
                 cross_copy(g, p).wait_recv()
-                recur(1, g, p, fixed + got_cross[g, p].astype(f32))
+                if g:
+                    other = got_cross[g, p].astype(f32)
+                else:
+                    if p == 0:
+                        remote(
+                            own_ahead, got_ahead, ahead_send, ahead_recv, mine, cross
+                        ).wait_recv()
+                    scale = jnp.concatenate([lead_scale[...]] * (piece // lanes), axis=1)
+                    other = got_ahead[0, p].astype(f32) + scale * got_ahead[1, p].astype(f32)
+                    other = jnp.concatenate([other, got_cross[0, p, lead:].astype(f32)], axis=0)
+                recur(1, g, p, fixed + other)
         with jax.named_scope("end%d" % g):
             small[3, g, 0] = jnp.concatenate(
                 [across(squares[g]), across(leans[g]), alphas[g][:2]], axis=0
             )
             small_start(3, g)
 
+    gather_start()
     for g in range(chunks):
         between(g)
         if g:
@@ -750,39 +870,37 @@
             ).astype(bf16).astype(f32)
             for m in range(member_rows):
                 final_ref[g * member_rows + m] = ending[m * seqs : (m + 1) * seqs].astype(bf16)
-        score_ref[...] = scores
+        score_ref[...] = scores[:, :members]
 
     with jax.named_scope("drain"):
         for hop in range(1, outer):
             relay_each(hop, lambda copy: copy.wait_send(), True)
         plane.wait_send()
-        for p in range(parts):
-            for slot in range(2):
-                part_copy(slot, p).wait_send()
-                over_copy(slot, p).wait_send()
-            hand_copy(p, twin).wait_send()
-        for g in range(chunks):
-            for p in range(parts):
-                pair_copy(g, 0, p).wait_send()
-                pair_copy(g, 1, p).wait_send()
-                cross_copy(g, p).wait_send()
-            for kind in range(4):
-                for r in range(3):
-                    small_copy(kind, g, r).wait_send()
-        in_buddy(mine).wait_send()
-        for hop in range(1, outer):
-            in_copy(hop, line).wait_send()
-            pass_copy(hop, twin).wait_send()
-        for hop in range(1, pop):
-            out_copy(hop, mine).wait_send()
+        remote(own_part, got_part, part_send, part_recv.at[0], mine, mate).wait_send()
+        remote(own_over, got_over, over_send, over_recv.at[0, 0], mine, cross).wait_send()
+        spot = table.at[:, pl.ds(0, share)]
+        remote(spot, spot, hand_send, hand_recv.at[0], buddy, me).wait_send()
+        remote(own_pair, got_pair, pair_send, pair_recv.at[0, 0], mine, mate).wait_send()
+        spot = own_cross.at[0, :, pl.ds(lead, rows - lead)]
+        remote(spot, spot, cross_send.at[0], cross_recv.at[0, 0], mine, cross).wait_send()
+        if chunks > 1:
+            spot = own_cross.at[pl.ds(1, chunks - 1)]
+            remote(spot, spot, cross_send.at[1], cross_recv.at[0, 0], mine, cross).wait_send()
+        remote(own_lead, got_lead, lead_send, lead_recv.at[0], mine, mate).wait_send()
+        remote(own_ahead, got_ahead, ahead_send, ahead_recv, mine, cross).wait_send()
+        spot = small.at[:, :, pl.ds(1, 3)]
+        remote(spot, spot, small_send, small_recv.at[0, 0], mine, mate).wait_send()
+        whole_in().wait_send()
+        whole_pass().wait_send()
+        whole_out().wait_send()
         half_copy(core).wait_send()
 
 
 cuts = 4
 
 
-def publish(final_ref, marks_ref, step_ref, final_out, score_out, step_out, sems):
-    copies = [pltpu.make_async_copy(final_ref, final_out, sems.at[2, 0])]
+def publish(final_ref, score_ref, step_ref, final_out, score_out, step_out, sems):
+    copies = []
     layers, width, _ = step_ref.shape
     cut = width // cuts
     for layer in range(layers):
@@ -793,9 +911,10 @@
                     step_ref.at[layer, at], step_out.at[layer, at], sems.at[layer, c]
                 )
             )
+    copies.append(pltpu.make_async_copy(final_ref, final_out, sems.at[layers, 0]))
+    copies.append(pltpu.make_async_copy(score_ref, score_out, sems.at[layers, 1]))
     for copy in copies:
         copy.start()
-    score_out[...] = marks_ref[:, : score_out.shape[1]]
     for copy in copies:
         copy.wait()
 
@@ -825,6 +944,7 @@
     rows = group * steps
     local = members * rank
     share = vocab * 3 // 8
+    lead = rows * 3 // 8
     dims = (pop, chunks, group, steps, member_rows, seqs, rank, width, full, coef, share)
     vmem = pl.BlockSpec(memory_space=pltpu.VMEM)
     smem = pl.BlockSpec(memory_space=pltpu.SMEM)
@@ -833,11 +953,11 @@
     piece = width // parts
     entries = vocab - share
     dma = pltpu.SemaphoreType.DMA
-    final_features, marks, step = pl.pallas_call(
+    final_features, scores, step = pl.pallas_call(
         functools.partial(policy_kernel, dims),
         out_shape=(
             pltpu.VMEM((members, seqs, width), bf16),
-            pltpu.VMEM((seqs, lanes), f32),
+            pltpu.VMEM((seqs, members), f32),
             pltpu.VMEM((layers, width, columns), f32),
         ),
         in_specs=[hbm, hbm, hbm, hbm, hbm, smem, hbm, hbm, hbm],
@@ -862,6 +982,12 @@
             pltpu.VMEM((chunks, 2, parts, rows, piece), bf16),
             pltpu.VMEM((chunks, parts, rows, piece), bf16),
             pltpu.VMEM((chunks, parts, rows, piece), bf16),
+            pltpu.VMEM((2, parts, lead, piece), bf16),
+            pltpu.VMEM((2, parts, lead, piece), bf16),
+            pltpu.VMEM((2, parts, lead, piece), bf16),
+            pltpu.VMEM((2, parts, lead, piece), bf16),
+            pltpu.VMEM((lead, width), bf16),
+            pltpu.VMEM((lead, lanes), f32),
             pltpu.VMEM((chunks, rows, width), f32),
             pltpu.VMEM((chunks, rows, width), bf16),
             pltpu.VMEM((chunks, rows, vocab), bf16),
@@ -878,30 +1004,35 @@
             pltpu.VMEM((16, width), bf16),
             pltpu.VMEM((chunks, 8, rows), f32),
             pltpu.VMEM((4, chunks, 4, 4, rows), f32),
-            dma((layers, 4)),
+            dma((3,)),
+            dma((2, parts)),
             dma((7,)),
+            dma,
+            dma((parts + 1,)),
+            dma,
             dma((2, parts)),
-            dma((2, parts)),
-            dma((2, parts)),
-            dma((2, parts)),
+            dma,
             dma((parts,)),
-            dma((parts,)),
-            dma((chunks, 2, parts)),
-            dma((chunks, 2, parts)),
+            dma,
+            dma((chunks, parts + 1)),
+            dma((2,)),
             dma((chunks, parts)),
-            dma((chunks, parts)),
-            dma((4, chunks, 3)),
-            dma((4, chunks, 3)),
-            dma((2, outer)),
-            dma((2, outer)),
+            dma,
+            dma((parts + 1,)),
+            dma,
+            dma,
+            dma,
+            dma((4, chunks)),
+            dma((2, outer - 1)),
+            dma((2, outer - 1)),
+            dma,
             dma,
             dma,
             dma((outer,)),
-            dma((outer,)),
-            dma((outer,)),
-            dma((outer,)),
-            dma((pop,)),
-            dma((pop,)),
+            dma,
+            dma,
+            dma,
+            dma,
             dma,
             dma,
             dma((2,)),
@@ -933,10 +1064,10 @@
             jax.ShapeDtypeStruct((layers, width, columns), f32),
         ),
         in_specs=[vmem, vmem, vmem],
-        out_specs=(hbm, vmem, hbm),
-        scratch_shapes=[dma((3, cuts))],
+        out_specs=(hbm, hbm, hbm),
+        scratch_shapes=[dma((layers + 1, cuts))],
         compiler_params=pltpu.CompilerParams(vmem_limit_bytes=1024 * 1024),
-    )(final_features, marks, step)
+    )(final_features, scores, step)
     return (final_features, scores.T, weight_step)
 
 

time: 68.5 us -> 64 us (0.934)
  Pallas kernels: 67.4 us -> 63 us
    pallas_call x1, Pallas kernels: 64.6 us -> 60.9 us  [shards(): pl.pallas_call(functools.partial(policy_kernel, dims), out_shape=(pltpu.V...]
where the time goes in v2:
time: 64 us; the launch traced here: 63.8 us
  Pallas kernels  63 us (98%)
  between operations  0.82 us (1%)
    pallas_call x1, Pallas kernels, shards(): pl.pallas_call(functools.partial(policy_kernel, dims), out_shape=(pltpu.V...  60.9 us
    pallas_call x1, Pallas kernels, shards(): pl.pallas_call(publish, out_shape=(jax.ShapeDtypeStruct((members, seqs, w...  2.13 us

profile of v2, /device:TPU:0, one launch (start us, length us, event | category | flops | bytes accessed | tf_op | source)
XLA Modules:
  0.0 63.8 jit_solution(87844866453253827)
XLA Ops:
  0.6 60.9 %shard_map.112 = (bf16[12,4,1024]{2,1,0:T(4,128)(2,1)S(1)}, f32[4,12]{1,0:T(4,128)S(1)}, f32[2,1024,512]{2,1,0:T(8,128)S(1)}) custom-call(s32[12,4,16]{2,1,0:T(4,128)} %ids_hbm.1, bf16[256,1024]{1,0:T(8,128)(2,1)} %embed_hbm.1, bf16[2,1024,4096]{2,1,0:T(8,128)(2,1)} %mix_ref.1, bf16[2,12,4,1024]{3,2,1,0:T(4,128)(2,1)} %fin_hbm.1, ...), custom_call_target="tpu_custom_call" | custom-call | tf_op jit(solution)/shard_map/pallas_call | solution.py:956
  61.5 2.1 %shard_map.113 = (bf16[12,4,1024]{2,1,0:T(4,128)(2,1)}, f32[4,12]{1,0:T(4,128)}, f32[2,1024,512]{2,1,0:T(8,128)}) custom-call(bf16[12,4,1024]{2,1,0:T(4,128)(2,1)S(1)} %get-tuple-element.9.final_ref, f32[4,12]{1,0:T(4,128)S(1)} %get-tuple-element.10.score_ref, f32[2,1024,512]{2,1,0:T(8,128)S(1)} %get-tuple-element.11.step_ref), custom_call_target="tpu_custom_call" | custom-call | tf_op jit(solution)/shard_map/pallas_call | solution.py:1059

commit v3 on v2

--- a/solution.py
+++ b/solution.py
@@ -58,7 +58,7 @@
     onehot_ref,
     fin_ref,
     fout_ref,
-    scaled,
+    shaped_ref,
     gin_ref,
     gout_ref,
     granks_ref,
@@ -70,7 +70,6 @@
     alphas,
     small,
     weight_sem,
-    column_sem,
     load_sem,
     part_send,
     part_recv,
@@ -80,6 +79,7 @@
     hand_recv,
     pair_send,
     pair_recv,
+    lone_recv,
     cross_send,
     cross_recv,
     lead_send,
@@ -94,6 +94,7 @@
     plane_recv,
     in_send,
     in_recv,
+    buddy_recv,
     pass_send,
     pass_recv,
     out_send,
@@ -103,7 +104,7 @@
     self_sem,
 ):
     pop, chunks, group, steps, member_rows, seqs, rank, width, full, coef, share = dims
-    parts = cross_recv.shape[1]
+    parts = hand_recv.shape[0]
     piece = width // parts
     halves = [slice(p * piece, (p + 1) * piece) for p in range(parts)]
     rows = group * steps
@@ -164,15 +165,7 @@
         return pltpu.make_async_copy(
             mix_ref.at[layer, :, pl.ds(start, width)],
             weights.at[slot],
-            weight_sem.at[2 if layer else slot - 2],
-        )
-
-    def column_copy(slot, p):
-        start = pl.multiple_of(blocks[slot] * width + p * piece, lanes)
-        return pltpu.make_async_copy(
-            mix_ref.at[0, :, pl.ds(start, piece)],
-            weights.at[slot, :, halves[p]],
-            column_sem.at[slot, p],
+            weight_sem.at[4 + slot // 2 if layer else slot],
         )
 
     loads = [
@@ -191,8 +184,7 @@
     ]
     loads[0].start()
     for slot in range(2):
-        for p in range(parts):
-            column_copy(slot, p).start()
+        weight_copy(0, slot).start()
     for copy in loads[1:3]:
         copy.start()
     weight_copy(0, 2).start()
@@ -323,14 +315,111 @@
             own_part.at[slot, p],
             got_part.at[slot, p],
             part_send,
-            part_recv.at[parts if slot else p],
+            part_recv.at[slot, p],
             mine,
             mate,
         )
 
-    def whole_part(slot):
-        return remote(
-            own_part.at[slot], got_part.at[slot], part_send, part_recv.at[parts], mine, mate
+    def own_rows(q):
+        return pl.ds(pl.multiple_of(q * local, local), local)
+
+    def in_copy(way, hop, source):
+        return remote(
+            fin_ref,
+            gin_ref.at[:, own_rows(at_line(source)), :],
+            in_send,
+            in_recv.at[way, hop - 1],
+            at_line(line + hop) if way == 0 else at_line(line - hop),
+            me,
+        )
+
+    def in_start(hop):
+        @pl.when(line + hop < outer)
+        def _():
+            in_copy(0, hop, line).start()
+
+        @pl.when(line >= hop)
+        def _():
+            in_copy(1, hop, line).start()
+
+    def in_pass(hop):
+        @pl.when(line >= hop)
+        def _():
+            in_copy(0, hop, line - hop).wait_recv()
+            pass_copy(line - hop, twin).start()
+
+        @pl.when(line + hop < outer)
+        def _():
+            in_copy(1, hop, line + hop).wait_recv()
+            pass_copy(line + hop, twin).start()
+
+    def in_buddy(source):
+        return remote(
+            fin_ref,
+            gin_ref.at[:, own_rows(source), :],
+            in_send,
+            buddy_recv,
+            buddy,
+            me,
+        )
+
+    def pass_copy(place, side_of):
+        at = own_rows(place * 2 + side_of)
+        return remote(
+            gin_ref.at[:, at, :],
+            gin_ref.at[:, at, :],
+            pass_send,
+            pass_recv,
+            buddy,
+            me,
+        )
+
+    def out_copy(hop, source):
+        target = lax.rem(mine + hop, pop)
+        cols = pl.multiple_of(target * columns, lanes)
+        return remote(
+            fout_ref.at[core, :, pl.ds(cols, columns)],
+            gout_ref.at[core, own_rows(source), :],
+            out_send,
+            out_recv,
+            target,
+            me,
+        )
+
+    def stretch(ref, count):
+        return ref.at[pl.ds(0, count * local), :]
+
+    def whole_out():
+        spot = stretch(gout_ref.at[core], pop - 1)
+        return remote(spot, spot, out_send, out_recv, buddy, me)
+
+    def whole_pass():
+        spot = gin_ref.at[:, pl.ds(0, (outer - 1) * local), :]
+        return remote(spot, spot, pass_send, pass_recv, buddy, me)
+
+    def whole_in():
+        spot = gin_ref.at[:, pl.ds(0, outer * local), :]
+        return remote(spot, spot, in_send, buddy_recv, buddy, me)
+
+    def half_copy(which):
+        return remote(
+            gout_ref.at[which],
+            gout_ref.at[which],
+            half_send,
+            half_recv,
+            mine,
+            mate,
+        )
+
+    def self_copies():
+        cols = pl.multiple_of(mine * columns, lanes)
+        return (
+            pltpu.make_async_copy(fin_ref, gin_ref.at[:, own_rows(mine), :], self_sem.at[0]),
+            pltpu.make_async_copy(
+                fout_ref.at[core, :, pl.ds(cols, columns)],
+                gout_ref.at[core, own_rows(mine), :],
+                self_sem.at[1],
+            ),
         )
 
     spans = (pl.ds(0, share), pl.ds(share, vocab - 2 * share))
@@ -362,11 +451,13 @@
         ).astype(bf16)
 
     def part_put(p):
-        column_copy(0, p).wait()
+        if p == 0:
+            weight_copy(0, 0).wait()
         own_part[0, p] = entry(0, p)
 
     def part_sum(p):
-        column_copy(1, p).wait()
+        if p == 0:
+            weight_copy(0, 1).wait()
         value = entry(1, p).astype(f32)
         part_copy(0, p).wait_recv()
         own_over[p] = (value + got_part[0, p].astype(f32)).astype(bf16)
@@ -420,17 +511,75 @@
         over_copy(1, p).start()
     with jax.named_scope("relay1"):
         relay_next(1)
+        in_start(1)
     with jax.named_scope("tab2"):
         weight_copy(0, 2).wait()
         for p in range(parts):
             own_part[1, p] = entry(2, p)
             part_copy(1, p).start()
         weight_copy(1, 2).start()
+    def both(h, p):
+        at = spans[h]
+        return (
+            mine_part[p, at].astype(f32) + got_part[1, p, at].astype(f32)
+        ) + got_over[p, at].astype(f32)
+
+    lead = lifted.shape[0]
+
+    def lead_pair(k, p):
+        return remote(
+            own_lead.at[k, p],
+            got_lead.at[k, p],
+            lead_send,
+            lead_recv.at[1 + p if k else 0],
+            mine,
+            mate,
+        )
+
+    def whole_lead():
+        return remote(own_lead.at[0], got_lead.at[0], lead_send, lead_recv.at[0], mine, mate)
+
+    def lead_cross(k, p):
+        return remote(
+            own_ahead.at[k, p], got_ahead.at[k, p], ahead_send, ahead_recv, mine, cross
+        )
+
+    def lead_rows(k):
+        return lifted[...] if k else hidden[0, :lead]
+
+    def lead_put(k, p):
+        if k == 0 and p == 0:
+            wait_weights(0)
+        own_lead[k, p] = jnp.dot(
+            lead_rows(k), weights[0, :, halves[p]], preferred_element_type=f32
+        ).astype(bf16)
+        lead_pair(k, p).start()
+
+    def lead_sum(k, p):
+        value = (
+            jnp.dot(lead_rows(k), weights[1, :, halves[p]], preferred_element_type=f32)
+            .astype(bf16)
+            .astype(f32)
+        )
+        if k:
+            lead_pair(k, p).wait_recv()
+        own_ahead[k, p] = (value + got_lead[k, p].astype(f32)).astype(bf16)
+        lead_cross(k, p).start()
+
+    def wait_weights(half):
+        spot = weights.at[pl.ds(2 * half, 2)]
+        pltpu.make_async_copy(spot, spot, weight_sem.at[4 + half]).wait()
+
+    with jax.named_scope("tabA"):
         weight_copy(0, 3).wait()
         for p in range(parts):
             mine_part[p] = entry(3, p)
+            part_copy(1, p).wait_recv()
+            over_copy(0, p).wait_recv()
+            table[p, pl.ds(pl.multiple_of(twin * share, share), share)] = both(0, p).astype(bf16)
+            hand_copy(p, twin).start()
         weight_copy(1, 3).start()
-
+        in_buddy(mine).start()
     with jax.named_scope("prep"):
         for copy in loads[3:]:
             copy.wait()
@@ -446,70 +595,20 @@
             jnp.where(index == 1, middle, jnp.where(index == 2, rest, 0.0)),
         ).astype(bf16)
 
-    def both(h, p):
-        at = spans[h]
-        return (
-            mine_part[p, at].astype(f32) + got_part[1, p, at].astype(f32)
-        ) + got_over[p, at].astype(f32)
-
-    lead = lifted.shape[0]
-
-    def lead_pair(k, p):
-        return remote(
-            own_lead.at[k, p],
-            got_lead.at[k, p],
-            lead_send,
-            lead_recv.at[1 + p if k else 0],
-            mine,
-            mate,
-        )
-
-    def whole_lead():
-        return remote(own_lead.at[0], got_lead.at[0], lead_send, lead_recv.at[0], mine, mate)
-
-    def lead_cross(k, p):
-        return remote(
-            own_ahead.at[k, p], got_ahead.at[k, p], ahead_send, ahead_recv, mine, cross
-        )
-
-    def lead_rows(k):
-        return lifted[...] if k else hidden[0, :lead]
-
-    def lead_put(k, p):
-        if k == 0 and p == 0:
-            wait_weights()
-        own_lead[k, p] = jnp.dot(
-            lead_rows(k), weights[0, :, halves[p]], preferred_element_type=f32
-        ).astype(bf16)
-        lead_pair(k, p).start()
-
-    def lead_sum(k, p):
-        value = (
-            jnp.dot(lead_rows(k), weights[1, :, halves[p]], preferred_element_type=f32)
-            .astype(bf16)
-            .astype(f32)
-        )
-        if k:
-            lead_pair(k, p).wait_recv()
-        own_ahead[k, p] = (value + got_lead[k, p].astype(f32)).astype(bf16)
-        lead_cross(k, p).start()
-
-    def wait_weights():
-        pltpu.make_async_copy(weights, weights, weight_sem.at[2]).wait()
-
-    with jax.named_scope("tabA"):
+    with jax.named_scope("leadx"):
         for p in range(parts):
-            over_copy(0, p).wait_recv()
-            if p == 0:
-                whole_part(1).wait_recv()
-            table[p, pl.ds(pl.multiple_of(twin * share, share), share)] = both(0, p).astype(bf16)
-            hand_copy(p, twin).start()
             lead_put(0, p)
-            if p == 1 and outer > 2:
-                relay_next(2)
     with jax.named_scope("lowready"):
         for g in range(chunks):
             low_ready(0, g)
+    with jax.named_scope("leads"):
+        whole_lead().wait_recv()
+        for p in range(parts):
+            lead_sum(0, p)
+    with jax.named_scope("relay2"):
+        if outer > 2:
+            relay_next(2)
+            in_start(2)
 
     def recur(layer, g, p, inputs):
         decay = decay_ref[layer : layer + 1, halves[p]]
@@ -551,17 +650,8 @@
         with jax.named_scope("tabB%d" % p):
             over_copy(1, p).wait_recv()
             table[p, 2 * share :] = both(1, p).astype(bf16)
-        with jax.named_scope("lead%d" % p):
-            if p == 0:
-                whole_lead().wait_recv()
-            lead_sum(0, p)
         with jax.named_scope("hand%d" % p):
             hand_copy(p, 1 - twin).wait_recv()
-        if p == 0:
-            with jax.named_scope("relay3"):
-                for hop in range(3, outer):
-                    relay_next(hop)
-                plane.start()
         with jax.named_scope("lz%d" % p):
             for g in range(chunks):
                 inputs = jnp.dot(
@@ -583,14 +673,19 @@
             own_pair.at[g, slot, p],
             got_pair.at[g, slot, p],
             pair_send,
-            pair_recv.at[g, parts if slot else p],
+            pair_recv.at[g, 1] if slot else lone_recv.at[p] if g == 0 else pair_recv.at[g, 0],
             mine,
             mate,
         )
 
-    def whole_pair(g):
-        return remote(
-            own_pair.at[g, 1], got_pair.at[g, 1], pair_send, pair_recv.at[g, parts], mine, mate
+    def whole_pair(g, slot):
+        return remote(
+            own_pair.at[g, slot],
+            got_pair.at[g, slot],
+            pair_send,
+            pair_recv.at[g, slot],
+            mine,
+            mate,
         )
 
     def cross_copy(g, p):
@@ -599,91 +694,20 @@
             own_cross.at[g, p, at],
             got_cross.at[g, p, at],
             cross_send.at[1 if g else 0],
-            cross_recv.at[g, p],
+            cross_recv.at[parts + g if g < chunks - 1 else p],
             mine,
             cross,
         )
 
-    def own_rows(q):
-        return pl.ds(pl.multiple_of(q * local, local), local)
-
-    def in_copy(hop, source):
-        return remote(
-            scaled,
-            gin_ref.at[:, own_rows(at_line(source)), :],
-            in_send,
-            in_recv.at[hop],
-            at_line(lax.rem(line + hop, outer)),
-            me,
-        )
-
-    def in_buddy(source):
-        return remote(
-            scaled,
-            gin_ref.at[:, own_rows(source), :],
-            in_send,
-            in_recv.at[0],
-            buddy,
-            me,
-        )
-
-    def pass_copy(hop, side_of):
-        at = own_rows(lax.rem(line + outer - hop, outer) * 2 + side_of)
-        return remote(
-            gin_ref.at[:, at, :],
-            gin_ref.at[:, at, :],
-            pass_send,
-            pass_recv,
-            buddy,
-            me,
-        )
-
-    def out_copy(hop, source):
-        target = lax.rem(mine + hop, pop)
-        cols = pl.multiple_of(target * columns, lanes)
-        return remote(
-            fout_ref.at[core, :, pl.ds(cols, columns)],
-            gout_ref.at[core, own_rows(source), :],
-            out_send,
-            out_recv,
-            target,
-            me,
-        )
-
-    def stretch(ref, count):
-        return ref.at[pl.ds(0, count * local), :]
-
-    def whole_out():
-        spot = stretch(gout_ref.at[core], pop - 1)
-        return remote(spot, spot, out_send, out_recv, buddy, me)
-
-    def whole_pass():
-        spot = gin_ref.at[:, pl.ds(0, (outer - 1) * local), :]
-        return remote(spot, spot, pass_send, pass_recv, buddy, me)
-
-    def whole_in():
-        spot = gin_ref.at[:, pl.ds(0, outer * local), :]
-        return remote(spot, spot, in_send, in_recv.at[0], buddy, me)
-
-    def half_copy(which):
-        return remote(
-            gout_ref.at[which],
-            gout_ref.at[which],
-            half_send,
-            half_recv,
+    def whole_cross(g):
+        at = pl.ds(0 if g else lead, rows if g else rows - lead)
+        return remote(
+            own_cross.at[g, :, at],
+            got_cross.at[g, :, at],
+            cross_send.at[1 if g else 0],
+            cross_recv.at[parts + g],
             mine,
-            mate,
-        )
-
-    def self_copies():
-        cols = pl.multiple_of(mine * columns, lanes)
-        return (
-            pltpu.make_async_copy(scaled, gin_ref.at[:, own_rows(mine), :], self_sem.at[0]),
-            pltpu.make_async_copy(
-                fout_ref.at[core, :, pl.ds(cols, columns)],
-                gout_ref.at[core, own_rows(mine), :],
-                self_sem.at[1],
-            ),
+            cross,
         )
 
     def shape_ranks():
@@ -702,29 +726,24 @@
         rank_mean = mean_of(shares)
         apart = jnp.where(kept, shares - rank_mean[None, None], 0.0)
         spread = mean_of(apart * apart) + spread_eps
-        own = rank_block((local, lanes), 0, rank).astype(f32) / members_all
-        shaped = (own - rank_mean) * lax.rsqrt(spread)
-        shaped = jnp.concatenate([shaped] * (width // lanes), axis=1)
-        for layer in range(layers):
-            scaled[layer] = (fin_ref[layer].astype(f32) * shaped).astype(bf16)
-
-    def gather_start():
-        with jax.named_scope("ranks"):
+        owner = lax.broadcasted_iota(jnp.int32, (local, lanes), 0) // rank
+        own = owner == lax.broadcasted_iota(jnp.int32, (local, lanes), 1)
+        for place in range(outer):
+            for side_of in range(2):
+                share_row = granks_ref[side_of, place, 0:1].astype(f32) / members_all
+                shaped = (share_row - rank_mean) * lax.rsqrt(spread)
+                shaped = jnp.where(own, jnp.broadcast_to(shaped, (local, lanes)), 0.0)
+                shaped = jnp.sum(shaped, axis=1, keepdims=True)
+                at = (place * 2 + side_of) * local
+                shaped_ref[at : at + local] = jnp.broadcast_to(shaped, (local, lanes))
+
+    def out_start():
+        with jax.named_scope("outs"):
             plane_in.wait_recv()
-            shape_ranks()
-            in_buddy(mine).start()
-            for hop in range(1, outer):
-                in_copy(hop, line).start()
             for hop in range(1, pop):
                 out_copy(hop, mine).start()
             for copy in self_copies():
                 copy.start()
-
-    def gather_pass(first, last):
-        with jax.named_scope("pass"):
-            for hop in range(first, min(last, outer)):
-                in_copy(hop, lax.rem(line + outer - hop, outer)).wait_recv()
-                pass_copy(hop, twin).start()
 
     def gather_half():
         with jax.named_scope("half"):
@@ -742,10 +761,13 @@
         with jax.named_scope("arrive_half"):
             half_copy(1 - core).wait_recv()
         with jax.named_scope("step"):
+            shape_ranks()
+            shaped = jnp.concatenate([shaped_ref[...]] * (tile // lanes), axis=1)
             for layer in range(layers):
                 for at in range(0, width, tile):
+                    factor = gin_ref[layer, :, at : at + tile].astype(f32)
                     value = lax.dot_general(
-                        gin_ref[layer, :, at : at + tile],
+                        (factor * shaped).astype(bf16),
                         gout_ref[layer],
                         (((0,), (0,)), ((), ())),
                         preferred_element_type=f32,
@@ -753,6 +775,8 @@
                     step_ref[layer, at : at + tile] = value * (members_all * rank) ** (-0.5)
 
     def between(g):
+        if g == 0:
+            wait_weights(1)
         with jax.named_scope("normed%d" % g):
             total = small_sum(2, g)[:1]
             scale = lax.rsqrt(total / full + norm_eps)
@@ -771,7 +795,10 @@
         with jax.named_scope("exch%d" % g):
             def summed(p):
                 value = product(1, p).astype(f32)
-                pair_copy(g, 0, p).wait_recv()
+                if g == 0:
+                    pair_copy(g, 0, p).wait_recv()
+                elif p == 0:
+                    whole_pair(g, 0).wait_recv()
                 total = (value + got_pair[g, 0, p].astype(f32)).astype(bf16)
                 if g:
                     own_cross[g, p] = total
@@ -782,7 +809,7 @@
             for p in range(parts):
                 own_pair[g, 0, p] = product(0, p)
                 pair_copy(g, 0, p).start()
-                if p:
+                if p and g == 0:
                     summed(p - 1)
             left = jnp.concatenate([factor_slice(fin_ref, 1, g, 0, width), heads[...]], axis=0)
             local_low = against(left, hidden[g])
@@ -790,7 +817,8 @@
             small_start(1, g)
             aligned = local_low[factor_rows : factor_rows + 8]
             alphas[g] = jnp.broadcast_to(jnp.sum(aligned, axis=0, keepdims=True), (8, rows))
-            summed(parts - 1)
+            for p in range(0 if g else parts - 1, parts):
+                summed(p)
             for p in range(parts):
                 own_pair[g, 1, p] = product(2, p)
                 pair_copy(g, 1, p).start()
@@ -803,11 +831,14 @@
         for p in range(parts):
             with jax.named_scope("l1_%d_%d" % (g, p)):
                 if p == 0:
-                    whole_pair(g).wait_recv()
+                    whole_pair(g, 1).wait_recv()
                 fixed = (
                     states[g, :, halves[p]] + got_pair[g, 1, p].astype(f32)
                 ) + correction(1, g, p)
-                cross_copy(g, p).wait_recv()
+                if g == chunks - 1:
+                    cross_copy(g, p).wait_recv()
+                elif p == 0:
+                    whole_cross(g).wait_recv()
                 if g:
                     other = got_cross[g, p].astype(f32)
                 else:
@@ -825,14 +856,25 @@
             )
             small_start(3, g)
 
-    gather_start()
+    with jax.named_scope("relay3"):
+        for hop in range(3, outer):
+            relay_next(hop)
+            in_start(hop)
+        plane.start()
+    with jax.named_scope("pass1"):
+        in_pass(1)
     for g in range(chunks):
         between(g)
-        if g:
-            gather_pass(g, g + 1)
+        if g == 0:
+            out_start()
+        with jax.named_scope("pass"):
+            for hop in range(g + 1, min(g + 2, outer) if g else 0):
+                in_pass(hop)
     for g in range(chunks):
         if g == chunks - 1:
-            gather_pass(chunks, outer)
+            with jax.named_scope("pass"):
+                for hop in range(chunks + 1, outer):
+                    in_pass(hop)
             gather_half()
             if g:
                 layer_one(g - 1)
@@ -876,16 +918,16 @@
         for hop in range(1, outer):
             relay_each(hop, lambda copy: copy.wait_send(), True)
         plane.wait_send()
-        remote(own_part, got_part, part_send, part_recv.at[0], mine, mate).wait_send()
+        remote(own_part, got_part, part_send, part_recv.at[0, 0], mine, mate).wait_send()
         remote(own_over, got_over, over_send, over_recv.at[0, 0], mine, cross).wait_send()
         spot = table.at[:, pl.ds(0, share)]
         remote(spot, spot, hand_send, hand_recv.at[0], buddy, me).wait_send()
         remote(own_pair, got_pair, pair_send, pair_recv.at[0, 0], mine, mate).wait_send()
         spot = own_cross.at[0, :, pl.ds(lead, rows - lead)]
-        remote(spot, spot, cross_send.at[0], cross_recv.at[0, 0], mine, cross).wait_send()
+        remote(spot, spot, cross_send.at[0], cross_recv.at[0], mine, cross).wait_send()
         if chunks > 1:
             spot = own_cross.at[pl.ds(1, chunks - 1)]
-            remote(spot, spot, cross_send.at[1], cross_recv.at[0, 0], mine, cross).wait_send()
+            remote(spot, spot, cross_send.at[1], cross_recv.at[0], mine, cross).wait_send()
         remote(own_lead, got_lead, lead_send, lead_recv.at[0], mine, mate).wait_send()
         remote(own_ahead, got_ahead, ahead_send, ahead_recv, mine, cross).wait_send()
         spot = small.at[:, :, pl.ds(1, 3)]
@@ -943,8 +985,8 @@
     group = member_rows * seqs
     rows = group * steps
     local = members * rank
-    share = vocab * 3 // 8
-    lead = rows * 3 // 8
+    share = vocab * 5 // 16
+    lead = rows * 5 // 16
     dims = (pop, chunks, group, steps, member_rows, seqs, rank, width, full, coef, share)
     vmem = pl.BlockSpec(memory_space=pltpu.VMEM)
     smem = pl.BlockSpec(memory_space=pltpu.SMEM)
@@ -993,7 +1035,7 @@
             pltpu.VMEM((chunks, rows, vocab), bf16),
             pltpu.VMEM((layers, local, width), bf16),
             pltpu.VMEM((layers, local, full), bf16),
-            pltpu.VMEM((layers, local, width), bf16),
+            pltpu.VMEM((pop * local, lanes), f32),
             pltpu.VMEM((layers, pop * local, width), bf16),
             pltpu.VMEM((layers, pop * local, columns), bf16),
             pltpu.VMEM((2, outer, 8, lanes), jnp.int32),
@@ -1004,19 +1046,19 @@
             pltpu.VMEM((16, width), bf16),
             pltpu.VMEM((chunks, 8, rows), f32),
             pltpu.VMEM((4, chunks, 4, 4, rows), f32),
-            dma((3,)),
+            dma((6,)),
+            dma((7,)),
+            dma,
             dma((2, parts)),
-            dma((7,)),
-            dma,
-            dma((parts + 1,)),
             dma,
             dma((2, parts)),
             dma,
             dma((parts,)),
             dma,
-            dma((chunks, parts + 1)),
+            dma((chunks, 2)),
+            dma((parts,)),
             dma((2,)),
-            dma((chunks, parts)),
+            dma((parts + chunks - 1,)),
             dma,
             dma((parts + 1,)),
             dma,
@@ -1028,7 +1070,8 @@
             dma,
             dma,
             dma,
-            dma((outer,)),
+            dma((2, outer - 1)),
+            dma,
             dma,
             dma,
             dma,

time: 64 us -> 62.6 us (0.978)
  Pallas kernels: 63 us -> 61.6 us
    pallas_call x1, Pallas kernels: 60.9 us -> 59.5 us  [shards(): pl.pallas_call(functools.partial(policy_kernel, dims), out_shape=(pltpu.V...]
where the time goes in v3:
time: 62.6 us; the launch traced here: 62.4 us
  Pallas kernels  61.6 us (98%)
  between operations  0.8 us (1%)
    pallas_call x1, Pallas kernels, shards(): pl.pallas_call(functools.partial(policy_kernel, dims), out_shape=(pltpu.V...  59.5 us
    pallas_call x1, Pallas kernels, shards(): pl.pallas_call(publish, out_shape=(jax.ShapeDtypeStruct((members, seqs, w...  2.13 us

profile of v3, /device:TPU:0, one launch (start us, length us, event | category | flops | bytes accessed | tf_op | source)
XLA Modules:
  0.0 62.4 jit_solution(7531325701024161072)
XLA Ops:
  0.6 59.5 %shard_map.112 = (bf16[12,4,1024]{2,1,0:T(4,128)(2,1)S(1)}, f32[4,12]{1,0:T(4,128)S(1)}, f32[2,1024,512]{2,1,0:T(8,128)S(1)}) custom-call(s32[12,4,16]{2,1,0:T(4,128)} %ids_hbm.1, bf16[256,1024]{1,0:T(8,128)(2,1)} %embed_hbm.1, bf16[2,1024,4096]{2,1,0:T(8,128)(2,1)} %mix_ref.1, bf16[2,12,4,1024]{3,2,1,0:T(4,128)(2,1)} %fin_hbm.1, ...), custom_call_target="tpu_custom_call" | custom-call | tf_op jit(solution)/shard_map/pallas_call | solution.py:998
  60.2 2.1 %shard_map.113 = (bf16[12,4,1024]{2,1,0:T(4,128)(2,1)}, f32[4,12]{1,0:T(4,128)}, f32[2,1024,512]{2,1,0:T(8,128)}) custom-call(bf16[12,4,1024]{2,1,0:T(4,128)(2,1)S(1)} %get-tuple-element.9.final_ref, f32[4,12]{1,0:T(4,128)S(1)} %get-tuple-element.10.score_ref, f32[2,1024,512]{2,1,0:T(8,128)S(1)} %get-tuple-element.11.step_ref), custom_call_target="tpu_custom_call" | custom-call | tf_op jit(solution)/shard_map/pallas_call | solution.py:1102

commit v4 on v3

--- a/solution.py
+++ b/solution.py
@@ -70,6 +70,7 @@
     alphas,
     small,
     weight_sem,
+    column_sem,
     load_sem,
     part_send,
     part_recv,
@@ -88,6 +89,8 @@
     ahead_recv,
     small_send,
     small_recv,
+    low_send,
+    low_recv,
     relay_send,
     relay_recv,
     plane_send,
@@ -165,13 +168,29 @@
         return pltpu.make_async_copy(
             mix_ref.at[layer, :, pl.ds(start, width)],
             weights.at[slot],
-            weight_sem.at[4 + slot // 2 if layer else slot],
+            weight_sem.at[2 + slot // 2 if layer else slot - 2],
+        )
+
+    def column_copy(slot, p):
+        start = pl.multiple_of(blocks[slot] * width + p * piece, lanes)
+        return pltpu.make_async_copy(
+            mix_ref.at[0, :, pl.ds(start, piece)],
+            weights.at[slot, :, halves[p]],
+            column_sem.at[slot, p],
         )
 
     loads = [
         pltpu.make_async_copy(src, dst, load_sem.at[i])
         for i, (src, dst) in enumerate(
             (
+                (
+                    embed_hbm.at[pl.ds(pl.multiple_of(twin * share, share), share)],
+                    rows_embed.at[pl.ds(0, share)],
+                ),
+                (
+                    embed_hbm.at[pl.ds(2 * share, embed_ref.shape[0] - 2 * share)],
+                    rows_embed.at[pl.ds(share, embed_ref.shape[0] - 2 * share)],
+                ),
                 (embed_hbm, embed_ref),
                 (ids_hbm, ids_ref),
                 (fin_hbm, fin_raw),
@@ -182,15 +201,10 @@
             )
         )
     ]
-    loads[0].start()
+    for copy in loads[:2]:
+        copy.start()
     for slot in range(2):
-        weight_copy(0, slot).start()
-    for copy in loads[1:3]:
-        copy.start()
-    weight_copy(0, 2).start()
-    weight_copy(0, 3).start()
-    for copy in loads[3:]:
-        copy.start()
+        column_copy(slot, 0).start()
 
     def rank_block(shape, axis, repeats):
         index = lax.broadcasted_iota(jnp.int32, shape, axis)
@@ -229,7 +243,7 @@
             small.at[kind, g, 0],
             small.at[kind, g, r + 1],
             small_send,
-            small_recv.at[kind, g],
+            small_recv.at[kind - 2, g],
             mine,
             others[r],
         )
@@ -240,8 +254,23 @@
 
     def small_sum(kind, g):
         arrived = small.at[kind, g, pl.ds(1, 3)]
-        remote(arrived, arrived, small_send, small_recv.at[kind, g], mine, mate).wait_recv()
+        remote(arrived, arrived, small_send, small_recv.at[kind - 2, g], mine, mate).wait_recv()
         return (small[kind, g, 0] + small[kind, g, 1]) + (small[kind, g, 2] + small[kind, g, 3])
+
+    def low_copy(layer, g, stage):
+        return remote(
+            small.at[layer, g, 2 * stage],
+            small.at[layer, g, 2 * stage + 1],
+            low_send,
+            low_recv.at[layer, stage, g],
+            mine,
+            mate if stage else cross,
+        )
+
+    def low_fold(layer, g):
+        low_copy(layer, g, 0).wait_recv()
+        small[layer, g, 2] = small[layer, g, 0] + small[layer, g, 1]
+        low_copy(layer, g, 1).start()
 
     def against(left, features):
         return lax.dot_general(
@@ -256,7 +285,8 @@
         small[layer, g, 0] = packed
 
     def low_ready(layer, g):
-        packed = small_sum(layer, g)
+        low_copy(layer, g, 1).wait_recv()
+        packed = small[layer, g, 2] + small[layer, g, 3]
         low = jnp.concatenate([packed] * member_rows, axis=0)
         low = jnp.where(mask, low, 0.0) * coef
         top = low.astype(bf16).astype(f32)
@@ -271,9 +301,11 @@
         )
         return jnp.dot(lows[g], right, preferred_element_type=f32)
 
-    loads[0].wait()
-    rows_embed[:share] = embed_ref[pl.ds(pl.multiple_of(twin * share, share), share), :]
-    rows_embed[share:] = embed_ref[2 * share :]
+    for copy in loads[:2]:
+        copy.wait()
+    for p in range(1, parts):
+        for slot in range(2):
+            column_copy(slot, p).start()
     def relay_copy(way, hop, source):
         return remote(
             granks_ref.at[twin, source],
@@ -451,22 +483,20 @@
         ).astype(bf16)
 
     def part_put(p):
-        if p == 0:
-            weight_copy(0, 0).wait()
+        column_copy(0, p).wait()
         own_part[0, p] = entry(0, p)
 
+    def part_make(p):
+        column_copy(1, p).wait()
+        own_over[p] = entry(1, p)
+
     def part_sum(p):
-        if p == 0:
-            weight_copy(0, 1).wait()
-        value = entry(1, p).astype(f32)
         part_copy(0, p).wait_recv()
-        own_over[p] = (value + got_part[0, p].astype(f32)).astype(bf16)
+        own_over[p] = (own_over[p].astype(f32) + got_part[0, p].astype(f32)).astype(bf16)
         over_copy(0, p).start()
 
-    early = 2
     with jax.named_scope("tab0"):
-        for p in range(early):
-            part_put(p)
+        part_put(0)
     with jax.named_scope("bar"):
         pl.semaphore_wait(
             barrier,
@@ -475,20 +505,26 @@
 
     relay_start(1)
     with jax.named_scope("tab1"):
-        for p in range(early):
-            part_copy(0, p).start()
-        for p in range(early, parts):
+        part_copy(0, 0).start()
+        for copy in loads[2:5]:
+            copy.start()
+        for slot in range(2, 4):
+            weight_copy(0, slot).start()
+        for copy in loads[5:]:
+            copy.start()
+        part_make(0)
+        for p in range(1, parts):
             part_put(p)
             part_copy(0, p).start()
-        for p in range(parts):
-            part_sum(p)
+            if p > 1:
+                part_make(p - 1)
+            part_sum(p - 1)
+        part_make(parts - 1)
+        part_sum(parts - 1)
         weight_copy(1, 0).start()
         weight_copy(1, 1).start()
-    loads[1].wait()
-    loads[2].wait()
-    unpack(fin_raw, fin_ref)
-
-    def begin(g, carry):
+    over_copy(1, 0).start()
+    def begin(g):
         tokens = jnp.concatenate(
             [ids_ref[g * member_rows + m] for m in range(member_rows)], axis=0
         )
@@ -500,88 +536,77 @@
         features = jnp.dot(onehot_ref[g], embed_ref[...], preferred_element_type=f32).astype(bf16)
         hidden[g] = features
         low_put(0, g, against(factor_slice(fin_ref, 0, g, 0, width), features))
-        return carry
-
-    with jax.named_scope("begin"):
-        lax.fori_loop(0, chunks, begin, 0)
-
-    for g in range(chunks):
-        small_start(0, g)
-    for p in range(parts):
-        over_copy(1, p).start()
-    with jax.named_scope("relay1"):
-        relay_next(1)
-        in_start(1)
+
+    def both(h, p):
+        at = spans[h]
+        return (
+            mine_part[p, at].astype(f32) + got_part[1, p, at].astype(f32)
+        ) + got_over[p, at].astype(f32)
+
+    def lead_pair(k):
+        return remote(
+            own_lead.at[k], got_lead.at[k], lead_send, lead_recv.at[k], mine, mate
+        )
+
+    def lead_cross(k):
+        return remote(own_ahead.at[k], got_ahead.at[k], ahead_send, ahead_recv, mine, cross)
+
+    def lead_dot(k, slot):
+        left = lifted[...] if k else hidden[0]
+        return jnp.dot(
+            left, weights[slot, :, halves[0]], preferred_element_type=f32
+        ).astype(bf16)
+
+    def lead_put(k):
+        own_lead[k] = lead_dot(k, 0)
+        lead_pair(k).start()
+
+    def lead_sum(k):
+        value = lead_dot(k, 1).astype(f32)
+        lead_pair(k).wait_recv()
+        own_ahead[k] = (value + got_lead[k].astype(f32)).astype(bf16)
+        lead_cross(k).start()
+
+    def wait_weights(half):
+        spot = weights.at[pl.ds(2 * half, 2)]
+        pltpu.make_async_copy(spot, spot, weight_sem.at[2 + half]).wait()
+
     with jax.named_scope("tab2"):
+        for copy in loads[2:5]:
+            copy.wait()
+        unpack(fin_raw, fin_ref)
         weight_copy(0, 2).wait()
         for p in range(parts):
             own_part[1, p] = entry(2, p)
             part_copy(1, p).start()
         weight_copy(1, 2).start()
-    def both(h, p):
-        at = spans[h]
-        return (
-            mine_part[p, at].astype(f32) + got_part[1, p, at].astype(f32)
-        ) + got_over[p, at].astype(f32)
-
-    lead = lifted.shape[0]
-
-    def lead_pair(k, p):
-        return remote(
-            own_lead.at[k, p],
-            got_lead.at[k, p],
-            lead_send,
-            lead_recv.at[1 + p if k else 0],
-            mine,
-            mate,
-        )
-
-    def whole_lead():
-        return remote(own_lead.at[0], got_lead.at[0], lead_send, lead_recv.at[0], mine, mate)
-
-    def lead_cross(k, p):
-        return remote(
-            own_ahead.at[k, p], got_ahead.at[k, p], ahead_send, ahead_recv, mine, cross
-        )
-
-    def lead_rows(k):
-        return lifted[...] if k else hidden[0, :lead]
-
-    def lead_put(k, p):
-        if k == 0 and p == 0:
-            wait_weights(0)
-        own_lead[k, p] = jnp.dot(
-            lead_rows(k), weights[0, :, halves[p]], preferred_element_type=f32
-        ).astype(bf16)
-        lead_pair(k, p).start()
-
-    def lead_sum(k, p):
-        value = (
-            jnp.dot(lead_rows(k), weights[1, :, halves[p]], preferred_element_type=f32)
-            .astype(bf16)
-            .astype(f32)
-        )
-        if k:
-            lead_pair(k, p).wait_recv()
-        own_ahead[k, p] = (value + got_lead[k, p].astype(f32)).astype(bf16)
-        lead_cross(k, p).start()
-
-    def wait_weights(half):
-        spot = weights.at[pl.ds(2 * half, 2)]
-        pltpu.make_async_copy(spot, spot, weight_sem.at[4 + half]).wait()
-
-    with jax.named_scope("tabA"):
-        weight_copy(0, 3).wait()
-        for p in range(parts):
+    with jax.named_scope("relay1"):
+        relay_next(1)
+        in_start(1)
+    weight_copy(0, 3).wait()
+    issued = 1
+    first = min(max(chunks - 1, 1), parts)
+    for p in range(parts):
+        if p < first:
+            with jax.named_scope("begin%d" % p):
+                begin(p)
+                low_copy(0, p, 0).start()
+            if issued < parts:
+                over_copy(1, issued).start()
+                issued += 1
+        with jax.named_scope("tabA%d" % p):
             mine_part[p] = entry(3, p)
             part_copy(1, p).wait_recv()
             over_copy(0, p).wait_recv()
-            table[p, pl.ds(pl.multiple_of(twin * share, share), share)] = both(0, p).astype(bf16)
+            at = pl.ds(pl.multiple_of(twin * share, share), share)
+            table[p, at] = both(0, p).astype(bf16)
             hand_copy(p, twin).start()
-        weight_copy(1, 3).start()
-        in_buddy(mine).start()
+    for p in range(issued, parts):
+        over_copy(1, p).start()
+    weight_copy(1, 3).start()
+    in_buddy(mine).start()
     with jax.named_scope("prep"):
-        for copy in loads[3:]:
+        for copy in loads[5:]:
             copy.wait()
         unpack(fout_raw, fout_ref)
         reward = reward_ref[...]
@@ -595,16 +620,16 @@
             jnp.where(index == 1, middle, jnp.where(index == 2, rest, 0.0)),
         ).astype(bf16)
 
+    wait_weights(0)
     with jax.named_scope("leadx"):
-        for p in range(parts):
-            lead_put(0, p)
-    with jax.named_scope("lowready"):
-        for g in range(chunks):
-            low_ready(0, g)
-    with jax.named_scope("leads"):
-        whole_lead().wait_recv()
-        for p in range(parts):
-            lead_sum(0, p)
+        lead_put(0)
+        for g in range(first, chunks):
+            begin(g)
+            low_copy(0, g, 0).start()
+        lead_sum(0)
+    with jax.named_scope("folds"):
+        for g in range(max(chunks - 1, 1)):
+            low_fold(0, g)
     with jax.named_scope("relay2"):
         if outer > 2:
             relay_next(2)
@@ -646,33 +671,56 @@
         small[2, g, 0] = jnp.broadcast_to(across(squares[g]), (4, rows))
         small_start(2, g)
 
-    for p in range(parts):
+    def complete(p):
         with jax.named_scope("tabB%d" % p):
             over_copy(1, p).wait_recv()
             table[p, 2 * share :] = both(1, p).astype(bf16)
         with jax.named_scope("hand%d" % p):
             hand_copy(p, 1 - twin).wait_recv()
-        with jax.named_scope("lz%d" % p):
-            for g in range(chunks):
-                inputs = jnp.dot(
-                    onehot_ref[g], table[p], preferred_element_type=f32
-                ) + correction(0, g, p)
-                recur(0, g, p, inputs)
-                if p == parts - 1:
-                    squares_start(g)
-                    if g == 0:
-                        with jax.named_scope("leadv"):
-                            lift = states[0, :lead] * gain_ref[0:1, :]
-                            lifted[...] = lift.astype(bf16)
-                            for q in range(parts):
-                                lead_put(1, q)
-                            for q in range(parts):
-                                lead_sum(1, q)
+
+    def layer_zero(g, p):
+        with jax.named_scope("lz%d_%d" % (g, p)):
+            inputs = jnp.dot(
+                onehot_ref[g], table[p], preferred_element_type=f32
+            ) + correction(0, g, p)
+            recur(0, g, p, inputs)
+
+    late = parts - 1
+
+    low_ready(0, 0)
+    for p in range(late):
+        complete(p)
+        layer_zero(0, p)
+    for g in range(1, chunks - 1):
+        low_ready(0, g)
+        for p in range(min(2, late)):
+            layer_zero(g, p)
+    if chunks > 1:
+        low_fold(0, chunks - 1)
+    complete(late)
+    layer_zero(0, late)
+    squares_start(0)
+    with jax.named_scope("leadv"):
+        lifted[...] = (states[0] * gain_ref[0:1, :]).astype(bf16)
+        lead_put(1)
+    for g in range(1, chunks - 1):
+        for p in range(min(2, late), late):
+            layer_zero(g, p)
+    if chunks > 1:
+        low_ready(0, chunks - 1)
+        for p in range(late):
+            layer_zero(chunks - 1, p)
+    with jax.named_scope("leadw"):
+        lead_sum(1)
+    for g in range(1, chunks):
+        layer_zero(g, late)
+        squares_start(g)
+
     def pair_copy(g, slot, p):
         return remote(
             own_pair.at[g, slot, p],
             got_pair.at[g, slot, p],
-            pair_send,
+            pair_send.at[2 if g else slot],
             pair_recv.at[g, 1] if slot else lone_recv.at[p] if g == 0 else pair_recv.at[g, 0],
             mine,
             mate,
@@ -682,17 +730,16 @@
         return remote(
             own_pair.at[g, slot],
             got_pair.at[g, slot],
-            pair_send,
+            pair_send.at[2 if g else slot],
             pair_recv.at[g, slot],
             mine,
             mate,
         )
 
     def cross_copy(g, p):
-        at = pl.ds(0 if g else lead, rows if g else rows - lead)
-        return remote(
-            own_cross.at[g, p, at],
-            got_cross.at[g, p, at],
+        return remote(
+            own_cross.at[g, p],
+            got_cross.at[g, p],
             cross_send.at[1 if g else 0],
             cross_recv.at[parts + g if g < chunks - 1 else p],
             mine,
@@ -700,10 +747,10 @@
         )
 
     def whole_cross(g):
-        at = pl.ds(0 if g else lead, rows if g else rows - lead)
-        return remote(
-            own_cross.at[g, :, at],
-            got_cross.at[g, :, at],
+        at = pl.ds(0 if g else 1, parts if g else late)
+        return remote(
+            own_cross.at[g, at],
+            got_cross.at[g, at],
             cross_send.at[1 if g else 0],
             cross_recv.at[parts + g],
             mine,
@@ -782,7 +829,7 @@
             scale = lax.rsqrt(total / full + norm_eps)
             scale = jnp.broadcast_to(scale, (lanes, rows)).T
             if g == 0:
-                lead_scale[...] = scale[:lead]
+                lead_scale[...] = scale
             scale = jnp.concatenate([scale] * (width // lanes), axis=1)
             gain = gain_ref[0:1, :]
             hidden[g] = (hidden[g].astype(f32) + states[g] * scale * gain).astype(bf16)
@@ -800,21 +847,18 @@
                 elif p == 0:
                     whole_pair(g, 0).wait_recv()
                 total = (value + got_pair[g, 0, p].astype(f32)).astype(bf16)
-                if g:
-                    own_cross[g, p] = total
-                else:
-                    own_cross[g, p, lead:] = total[lead:]
+                own_cross[g, p] = total
                 cross_copy(g, p).start()
 
-            for p in range(parts):
+            for p in range(0 if g else 1, parts):
                 own_pair[g, 0, p] = product(0, p)
                 pair_copy(g, 0, p).start()
-                if p and g == 0:
+                if p > 1 and g == 0:
                     summed(p - 1)
             left = jnp.concatenate([factor_slice(fin_ref, 1, g, 0, width), heads[...]], axis=0)
             local_low = against(left, hidden[g])
             low_put(1, g, local_low[:factor_rows])
-            small_start(1, g)
+            low_copy(1, g, 0).start()
             aligned = local_low[factor_rows : factor_rows + 8]
             alphas[g] = jnp.broadcast_to(jnp.sum(aligned, axis=0, keepdims=True), (8, rows))
             for p in range(0 if g else parts - 1, parts):
@@ -835,20 +879,16 @@
                 fixed = (
                     states[g, :, halves[p]] + got_pair[g, 1, p].astype(f32)
                 ) + correction(1, g, p)
-                if g == chunks - 1:
-                    cross_copy(g, p).wait_recv()
-                elif p == 0:
-                    whole_cross(g).wait_recv()
-                if g:
+                if g == 0 and p == 0:
+                    remote(own_ahead, got_ahead, ahead_send, ahead_recv, mine, cross).wait_recv()
+                    scale = jnp.concatenate([lead_scale[...]] * (piece // lanes), axis=1)
+                    other = got_ahead[0].astype(f32) + scale * got_ahead[1].astype(f32)
+                else:
+                    if g == chunks - 1:
+                        cross_copy(g, p).wait_recv()
+                    elif p == (0 if g else 1):
+                        whole_cross(g).wait_recv()
                     other = got_cross[g, p].astype(f32)
-                else:
-                    if p == 0:
-                        remote(
-                            own_ahead, got_ahead, ahead_send, ahead_recv, mine, cross
-                        ).wait_recv()
-                    scale = jnp.concatenate([lead_scale[...]] * (piece // lanes), axis=1)
-                    other = got_ahead[0, p].astype(f32) + scale * got_ahead[1, p].astype(f32)
-                    other = jnp.concatenate([other, got_cross[0, p, lead:].astype(f32)], axis=0)
                 recur(1, g, p, fixed + other)
         with jax.named_scope("end%d" % g):
             small[3, g, 0] = jnp.concatenate(
@@ -871,16 +911,19 @@
             for hop in range(g + 1, min(g + 2, outer) if g else 0):
                 in_pass(hop)
     for g in range(chunks):
-        if g == chunks - 1:
+        if g < chunks - 1:
+            low_fold(1, g)
+        else:
             with jax.named_scope("pass"):
                 for hop in range(chunks + 1, outer):
                     in_pass(hop)
             gather_half()
             if g:
                 layer_one(g - 1)
+            low_fold(1, g)
             step_make()
             layer_one(g)
-        elif g < chunks - 2:
+        if g < chunks - 2:
             layer_one(g)
 
     lane = lax.broadcasted_iota(jnp.int32, (seqs, lanes), 1)
@@ -922,15 +965,23 @@
         remote(own_over, got_over, over_send, over_recv.at[0, 0], mine, cross).wait_send()
         spot = table.at[:, pl.ds(0, share)]
         remote(spot, spot, hand_send, hand_recv.at[0], buddy, me).wait_send()
-        remote(own_pair, got_pair, pair_send, pair_recv.at[0, 0], mine, mate).wait_send()
-        spot = own_cross.at[0, :, pl.ds(lead, rows - lead)]
+        spot = own_pair.at[0, 0, pl.ds(1, late)]
+        remote(spot, spot, pair_send.at[0], pair_recv.at[0, 0], mine, mate).wait_send()
+        spot = own_pair.at[0, 1]
+        remote(spot, spot, pair_send.at[1], pair_recv.at[0, 0], mine, mate).wait_send()
+        spot = own_cross.at[0, pl.ds(1, late)]
         remote(spot, spot, cross_send.at[0], cross_recv.at[0], mine, cross).wait_send()
+        if chunks > 1:
+            spot = own_pair.at[pl.ds(1, chunks - 1)]
+            remote(spot, spot, pair_send.at[2], pair_recv.at[0, 0], mine, mate).wait_send()
         if chunks > 1:
             spot = own_cross.at[pl.ds(1, chunks - 1)]
             remote(spot, spot, cross_send.at[1], cross_recv.at[0], mine, cross).wait_send()
         remote(own_lead, got_lead, lead_send, lead_recv.at[0], mine, mate).wait_send()
         remote(own_ahead, got_ahead, ahead_send, ahead_recv, mine, cross).wait_send()
-        spot = small.at[:, :, pl.ds(1, 3)]
+        spot = small.at[pl.ds(0, 2), :, pl.ds(0, 2)]
+        remote(spot, spot, low_send, low_recv.at[0, 0, 0], mine, mate).wait_send()
+        spot = small.at[pl.ds(2, 2), :, pl.ds(1, 3)]
         remote(spot, spot, small_send, small_recv.at[0, 0], mine, mate).wait_send()
         whole_in().wait_send()
         whole_pass().wait_send()
@@ -938,7 +989,7 @@
         half_copy(core).wait_send()
 
 
-cuts = 4
+cuts = 2
 
 
 def publish(final_ref, score_ref, step_ref, final_out, score_out, step_out, sems):
@@ -986,7 +1037,6 @@
     rows = group * steps
     local = members * rank
     share = vocab * 5 // 16
-    lead = rows * 5 // 16
     dims = (pop, chunks, group, steps, member_rows, seqs, rank, width, full, coef, share)
     vmem = pl.BlockSpec(memory_space=pltpu.VMEM)
     smem = pl.BlockSpec(memory_space=pltpu.SMEM)
@@ -1024,12 +1074,12 @@
             pltpu.VMEM((chunks, 2, parts, rows, piece), bf16),
             pltpu.VMEM((chunks, parts, rows, piece), bf16),
             pltpu.VMEM((chunks, parts, rows, piece), bf16),
-            pltpu.VMEM((2, parts, lead, piece), bf16),
-            pltpu.VMEM((2, parts, lead, piece), bf16),
-            pltpu.VMEM((2, parts, lead, piece), bf16),
-            pltpu.VMEM((2, parts, lead, piece), bf16),
-            pltpu.VMEM((lead, width), bf16),
-            pltpu.VMEM((lead, lanes), f32),
+            pltpu.VMEM((2, rows, piece), bf16),
+            pltpu.VMEM((2, rows, piece), bf16),
+            pltpu.VMEM((2, rows, piece), bf16),
+            pltpu.VMEM((2, rows, piece), bf16),
+            pltpu.VMEM((rows, width), bf16),
+            pltpu.VMEM((rows, lanes), f32),
             pltpu.VMEM((chunks, rows, width), f32),
             pltpu.VMEM((chunks, rows, width), bf16),
             pltpu.VMEM((chunks, rows, vocab), bf16),
@@ -1046,25 +1096,28 @@
             pltpu.VMEM((16, width), bf16),
             pltpu.VMEM((chunks, 8, rows), f32),
             pltpu.VMEM((4, chunks, 4, 4, rows), f32),
-            dma((6,)),
-            dma((7,)),
-            dma,
+            dma((4,)),
             dma((2, parts)),
+            dma((9,)),
             dma,
             dma((2, parts)),
             dma,
+            dma((2, parts)),
+            dma,
             dma((parts,)),
-            dma,
+            dma((3,)),
             dma((chunks, 2)),
             dma((parts,)),
             dma((2,)),
             dma((parts + chunks - 1,)),
             dma,
-            dma((parts + 1,)),
-            dma,
-            dma,
-            dma,
-            dma((4, chunks)),
+            dma((2,)),
+            dma,
+            dma,
+            dma,
+            dma((2, chunks)),
+            dma,
+            dma((2, 2, chunks)),
             dma((2, outer - 1)),
             dma((2, outer - 1)),
             dma,

time: 62.6 us -> 62 us (level)
  no operation moved by 1% of the time
where the time goes in v4:
time: 62 us; the launch traced here: 61.9 us
  Pallas kernels  61.1 us (99%)
  between operations  0.8 us (1%)
    pallas_call x1, Pallas kernels, shards(): pl.pallas_call(functools.partial(policy_kernel, dims), out_shape=(pltpu.V...  59 us
    pallas_call x1, Pallas kernels, shards(): pl.pallas_call(publish, out_shape=(jax.ShapeDtypeStruct((members, seqs, w...  2.08 us

profile of v4, /device:TPU:0, one launch (start us, length us, event | category | flops | bytes accessed | tf_op | source)
XLA Modules:
  0.0 61.9 jit_solution(11556759019086627898)
XLA Ops:
  0.6 59.0 %shard_map.112 = (bf16[12,4,1024]{2,1,0:T(4,128)(2,1)S(1)}, f32[4,12]{1,0:T(4,128)S(1)}, f32[2,1024,512]{2,1,0:T(8,128)S(1)}) custom-call(s32[12,4,16]{2,1,0:T(4,128)} %ids_hbm.1, bf16[256,1024]{1,0:T(8,128)(2,1)} %embed_hbm.1, bf16[2,1024,4096]{2,1,0:T(8,128)(2,1)} %mix_ref.1, bf16[2,12,4,1024]{3,2,1,0:T(4,128)(2,1)} %fin_hbm.1, ...), custom_call_target="tpu_custom_call" | custom-call | tf_op jit(solution)/shard_map/pallas_call | solution.py:1048
  59.7 2.1 %shard_map.113 = (bf16[12,4,1024]{2,1,0:T(4,128)(2,1)}, f32[4,12]{1,0:T(4,128)}, f32[2,1024,512]{2,1,0:T(8,128)}) custom-call(bf16[12,4,1024]{2,1,0:T(4,128)(2,1)S(1)} %get-tuple-element.9.final_ref, f32[4,12]{1,0:T(4,128)S(1)} %get-tuple-element.10.score_ref, f32[2,1024,512]{2,1,0:T(8,128)S(1)} %get-tuple-element.11.step_ref), custom_call_target="tpu_custom_call" | custom-call | tf_op jit(solution)/shard_map/pallas_call | solution.py:1155

commit v5 on v4

--- a/solution.py
+++ b/solution.py
@@ -587,6 +587,13 @@
     issued = 1
     first = min(max(chunks - 1, 1), parts)
     for p in range(parts):
+        with jax.named_scope("tabA%d" % p):
+            mine_part[p] = entry(3, p)
+            part_copy(1, p).wait_recv()
+            over_copy(0, p).wait_recv()
+            at = pl.ds(pl.multiple_of(twin * share, share), share)
+            table[p, at] = both(0, p).astype(bf16)
+            hand_copy(p, twin).start()
         if p < first:
             with jax.named_scope("begin%d" % p):
                 begin(p)
@@ -594,13 +601,6 @@
             if issued < parts:
                 over_copy(1, issued).start()
                 issued += 1
-        with jax.named_scope("tabA%d" % p):
-            mine_part[p] = entry(3, p)
-            part_copy(1, p).wait_recv()
-            over_copy(0, p).wait_recv()
-            at = pl.ds(pl.multiple_of(twin * share, share), share)
-            table[p, at] = both(0, p).astype(bf16)
-            hand_copy(p, twin).start()
     for p in range(issued, parts):
         over_copy(1, p).start()
     weight_copy(1, 3).start()

time: 62 us -> 61.5 us (level)
  no operation moved by 1% of the time
where the time goes in v5:
time: 61.5 us; the launch traced here: 61.4 us
  Pallas kernels  60.6 us (99%)
  between operations  0.8 us (1%)
    pallas_call x1, Pallas kernels, shards(): pl.pallas_call(functools.partial(policy_kernel, dims), out_shape=(pltpu.V...  58.5 us
    pallas_call x1, Pallas kernels, shards(): pl.pallas_call(publish, out_shape=(jax.ShapeDtypeStruct((members, seqs, w...  2.08 us

profile of v5, /device:TPU:0, one launch (start us, length us, event | category | flops | bytes accessed | tf_op | source)
XLA Modules:
  0.0 61.4 jit_solution(14937613686214816025)
XLA Ops:
  0.6 58.5 %shard_map.112 = (bf16[12,4,1024]{2,1,0:T(4,128)(2,1)S(1)}, f32[4,12]{1,0:T(4,128)S(1)}, f32[2,1024,512]{2,1,0:T(8,128)S(1)}) custom-call(s32[12,4,16]{2,1,0:T(4,128)} %ids_hbm.1, bf16[256,1024]{1,0:T(8,128)(2,1)} %embed_hbm.1, bf16[2,1024,4096]{2,1,0:T(8,128)(2,1)} %mix_ref.1, bf16[2,12,4,1024]{3,2,1,0:T(4,128)(2,1)} %fin_hbm.1, ...), custom_call_target="tpu_custom_call" | custom-call | tf_op jit(solution)/shard_map/pallas_call | solution.py:1048
  59.2 2.1 %shard_map.113 = (bf16[12,4,1024]{2,1,0:T(4,128)(2,1)}, f32[4,12]{1,0:T(4,128)}, f32[2,1024,512]{2,1,0:T(8,128)}) custom-call(bf16[12,4,1024]{2,1,0:T(4,128)(2,1)S(1)} %get-tuple-element.9.final_ref, f32[4,12]{1,0:T(4,128)S(1)} %get-tuple-element.10.score_ref, f32[2,1024,512]{2,1,0:T(8,128)S(1)} %get-tuple-element.11.step_ref), custom_call_target="tpu_custom_call" | custom-call | tf_op jit(solution)/shard_map/pallas_call | solution.py:1155

commit v6 on v5

--- a/solution.py
+++ b/solution.py
@@ -693,7 +693,7 @@
         layer_zero(0, p)
     for g in range(1, chunks - 1):
         low_ready(0, g)
-        for p in range(min(2, late)):
+        for p in range(min(1, late)):
             layer_zero(g, p)
     if chunks > 1:
         low_fold(0, chunks - 1)
@@ -704,7 +704,7 @@
         lifted[...] = (states[0] * gain_ref[0:1, :]).astype(bf16)
         lead_put(1)
     for g in range(1, chunks - 1):
-        for p in range(min(2, late), late):
+        for p in range(min(1, late), late):
             layer_zero(g, p)
     if chunks > 1:
         low_ready(0, chunks - 1)

time: 61.5 us -> 61.5 us (level)
  no operation moved by 1% of the time
where the time goes in v6:
time: 61.5 us; the launch traced here: 61.4 us
  Pallas kernels  60.6 us (99%)
  between operations  0.8 us (1%)
    pallas_call x1, Pallas kernels, shards(): pl.pallas_call(functools.partial(policy_kernel, dims), out_shape=(pltpu.V...  58.5 us
    pallas_call x1, Pallas kernels, shards(): pl.pallas_call(publish, out_shape=(jax.ShapeDtypeStruct((members, seqs, w...  2.08 us

profile of v6, /device:TPU:0, one launch (start us, length us, event | category | flops | bytes accessed | tf_op | source)
XLA Modules:
  0.0 61.4 jit_solution(6234776895603106702)
XLA Ops:
  0.6 58.5 %shard_map.112 = (bf16[12,4,1024]{2,1,0:T(4,128)(2,1)S(1)}, f32[4,12]{1,0:T(4,128)S(1)}, f32[2,1024,512]{2,1,0:T(8,128)S(1)}) custom-call(s32[12,4,16]{2,1,0:T(4,128)} %ids_hbm.1, bf16[256,1024]{1,0:T(8,128)(2,1)} %embed_hbm.1, bf16[2,1024,4096]{2,1,0:T(8,128)(2,1)} %mix_ref.1, bf16[2,12,4,1024]{3,2,1,0:T(4,128)(2,1)} %fin_hbm.1, ...), custom_call_target="tpu_custom_call" | custom-call | tf_op jit(solution)/shard_map/pallas_call | solution.py:1048
  59.2 2.1 %shard_map.113 = (bf16[12,4,1024]{2,1,0:T(4,128)(2,1)}, f32[4,12]{1,0:T(4,128)}, f32[2,1024,512]{2,1,0:T(8,128)}) custom-call(bf16[12,4,1024]{2,1,0:T(4,128)(2,1)S(1)} %get-tuple-element.9.final_ref, f32[4,12]{1,0:T(4,128)S(1)} %get-tuple-element.10.score_ref, f32[2,1024,512]{2,1,0:T(8,128)S(1)} %get-tuple-element.11.step_ref), custom_call_target="tpu_custom_call" | custom-call | tf_op jit(solution)/shard_map/pallas_call | solution.py:1155
